TPU v7x, 32 devices: a whole 2x2x4 slice. The times are simulated.
32 devices in a mesh: gx: 4 (over z), gy: 4 (over y, core), gz: 2 (over x).
Axes of the slice: x: 2, y: 2, z: 4, core: 2. Of those that a mesh axis runs over, the one named last changes fastest.
Arguments:
- point_data: float32 [1, 6, 16384], P(None, None, ('gx', 'gy', 'gz')), may hold values from -1 to 1
- neighbours: int32 [1, 64, 64, 64, 32], P(None, 'gx', 'gy', 'gz'), may hold values from 0 to 16383, as said below
- counts: int32 [1, 64, 64, 64], P(None, 'gx', 'gy', 'gz'), may hold values from 1 to 32, as said below
- kernel_in: bfloat16 [6, 80], replicated, may hold values from -2.5 to 2.5
- kernel_mid: bfloat16 [80, 80], replicated, may hold values from -0.625 to 0.625
- kernel_out: bfloat16 [80, 64], replicated, may hold values from -0.625 to 0.625
- spectral: bfloat16 [2, 16, 16, 16, 64, 64], P(None, 'gz', 'gx', 'gy'), may hold values from -48 to 48
- skip_weight: bfloat16 [64, 64], replicated, may hold values from -0.75 to 0.75
Outputs:
- latent_out: float32 [1, 64, 64, 64, 64], P(None, 'gx', 'gy', 'gz')
Inputs may be any that keep to these rules, and one draw needn't show every extreme that they name: `neighbours`: points are owned by location: point j of a geometry belongs to the device at position j // 512 in the order gx, gy, gz. Every neighbour of a node is owned by the node's own device or by a device whose gx, gy and gz indices each differ from it by at most one. Slots s >= counts of the node are padding that names some point all the same. `counts`: on every device some node of every geometry has all 32 slots valid.
All inputs are finite; a program needn't handle non-finite values.
Results may differ from a plain program's by a relative error of at most 0.02.
Values may be sent and summed in bfloat16 or wider, within the bound.
A program may use at most 128 MiB of HBM per device.

v0:
```python
import functools
import math

import jax
import jax.numpy as jnp
import numpy as np
from jax import lax
from jax.experimental import pallas as pl
from jax.experimental.pallas import tpu as pltpu
from jax.sharding import PartitionSpec as P

GRID = 64
MODES = 16
NB = 32


HIGH = lax.Precision.HIGH
NORM_FLOOR = 1.0


def beside(cells, axis, dim):
    count = lax.axis_size(axis)
    turn = lambda by: lax.ppermute(cells, axis, [(i, (i + by) % count) for i in range(count)])
    if count == 1:
        return cells
    if count == 2:
        return jnp.concatenate([cells, turn(1)], axis=dim)
    return jnp.concatenate([turn(1), cells, turn(-1)], axis=dim)


def offset(owner, axis):
    count = lax.axis_size(axis)
    return (owner - lax.axis_index(axis) + (1 if count > 2 else 0)) % count, min(count, 3)


def tables(length, keep_count, centred):
    position = jnp.arange(length, dtype=jnp.int32)
    frequency = jnp.arange(keep_count, dtype=jnp.int32)
    if centred:
        frequency = jnp.where(
            frequency < keep_count // 2, frequency, frequency + length - keep_count
        )
    phases = frequency[:, None] * position[None, :] % length
    angles = phases.astype(jnp.float32) * (2.0 * math.pi / length)
    return (jnp.cos(angles), jnp.sin(angles))


def third_weights(cos_table, sin_table, length):
    factor = (
        jnp.where(jnp.arange(cos_table.shape[0]) == 0, 1.0, 2.0).astype(jnp.float32)[:, None]
        / length**3
    )
    return (cos_table * factor, sin_table * factor)


def contract(pattern, operand, table):
    return jnp.einsum(pattern, operand, table, precision=HIGH)


def forward_real(values, cos_table, sin_table, pattern):
    return (contract(pattern, values, cos_table), -contract(pattern, values, sin_table))


def forward_complex(real_part, imag_part, cos_table, sin_table, pattern):
    new_real = contract(pattern, real_part, cos_table) + contract(pattern, imag_part, sin_table)
    new_imag = contract(pattern, imag_part, cos_table) - contract(pattern, real_part, sin_table)
    return (new_real, new_imag)


def inverse_complex(real_part, imag_part, cos_table, sin_table, pattern):
    new_real = contract(pattern, real_part, cos_table) - contract(pattern, imag_part, sin_table)
    new_imag = contract(pattern, real_part, sin_table) + contract(pattern, imag_part, cos_table)
    return (new_real, new_imag)


def inverse_real(real_part, imag_part, cos_table, sin_table, pattern):
    return contract(pattern, real_part, cos_table) - contract(pattern, imag_part, sin_table)


SUB = 8
LANES = 128

SCALE = 0.035677408136300125 ** (-1.0 / 3.0)
SHIFT = 0.7978845608028654 * SCALE

def gelu2(y):
    return y + y * jnp.tanh(y * (y * y + jnp.asarray(SHIFT, y.dtype)))

def pick(leaf, bits, low, high, level):
    if high - low == 1:
        return leaf(low)
    half = 1 << (level - 1)
    if low + half >= high:
        return pick(leaf, bits, low, high, level - 1)
    a = pick(leaf, bits, low, low + half, level - 1)
    b = pick(leaf, bits, low + half, high, level - 1)
    return jnp.where(bits[level - 1], b, a)

def encoder_kernel(codes_ref, counts_ref, centres_ref, table_ref, first_ref, mid_ref, last_ref, out_ref, acc_ref, grouped, dt=jnp.bfloat16, per=2):
    slots, rows = codes_ref.shape[0:2]
    groups = rows // SUB
    words, table_rows = table_ref.shape[0:2]
    units = mid_ref.shape[0]
    channels = last_ref.shape[0]
    depth = max(1, (table_rows - 1).bit_length())
    acc_ref[...] = jnp.zeros_like(acc_ref)
    counts = [counts_ref[SUB*g:SUB*(g+1), :] for g in range(groups)]
    scale = 1.0 / (32767.0 * SCALE)
    def pairs(i):
        out = []
        for k in range(per):
            s = i * per + k
            stacks = []
            for g in range(groups):
                code = codes_ref[s, SUB*g:SUB*(g+1), :]
                lane = code & (LANES - 1)
                bits = [(code & (LANES << b)) != 0 for b in range(depth)]
                live = s < counts[g]
                vals = []
                for w in range(words):
                    leaf = lambda r: jnp.take_along_axis(
                        jnp.broadcast_to(table_ref[w, r:r+1, :], (SUB, LANES)), lane, axis=1, mode="promise_in_bounds")
                    word = pick(leaf, bits, 0, table_rows, depth)
                    vals += [word >> 16, (word & 65535) - 32768]
                parts = []
                for v in range(6):
                    x = vals[v].astype(jnp.float32) * scale
                    if v < 3:
                        x = x - centres_ref[v, SUB*g:SUB*(g+1), :]
                    parts.append(jnp.where(live, x, 0.0))
                stacks.append(jnp.concatenate(parts, axis=0).astype(jnp.bfloat16))
            out.append(jnp.concatenate(stacks, axis=1))
        return out
    def step(i, stacks):
        h2s = []
        for k in range(per):
            z1 = jnp.dot(first_ref[...], stacks[k], preferred_element_type=jnp.float32)
            h1 = gelu2(z1.astype(dt)).astype(jnp.bfloat16)
            wide = jnp.concatenate([h1[units*r:units*(r+1)] for r in range(SUB)], axis=1)
            z2 = jnp.dot(mid_ref[...], wide, preferred_element_type=jnp.float32)
            h2s.append(gelu2(z2.astype(dt)).astype(jnp.bfloat16))
        hidden = jnp.concatenate(h2s, axis=0)
        acc_ref[...] += jnp.dot(last_ref[...], hidden, preferred_element_type=jnp.float32)
        return pairs(jnp.minimum(i + 1, slots // per - 1))
    lax.fori_loop(0, slots // per, step, pairs(0))
    done = {}
    for r in range(SUB):
        for g in range(groups):
            at = (r * groups + g) * LANES
            row = SUB * g + r
            done[row] = acc_ref[:, at:at+LANES] * SCALE / counts_ref[row:row+1, :].astype(jnp.float32)
            if not grouped:
                out_ref[row] = done[row]
    if grouped:
        for q in range(channels // SUB):
            out_ref[q] = jnp.concatenate(
                [done[row][SUB * q : SUB * (q + 1)] for row in range(rows)], axis=0
            ).astype(jnp.bfloat16)

def encode(codes, counts, centres, table, kernel_in, kernel_mid, kernel_out, grouped, dt=jnp.bfloat16, per=2):
    slots, rows = codes.shape[0:2]
    units, channels = kernel_out.shape
    block = min(16, rows)
    w1 = kernel_in.T.astype(jnp.float32)
    first = jnp.einsum("hv,rq->rhvq", w1, jnp.eye(SUB, dtype=jnp.float32)).reshape(SUB*units, 6*SUB).astype(jnp.bfloat16)
    mid = (kernel_mid.T * 0.5).astype(jnp.bfloat16)
    last = jnp.concatenate([(kernel_out.T * 0.5).astype(jnp.bfloat16)]*per, axis=1)
    whole = lambda a: pl.BlockSpec(a.shape, lambda i: (0,)*a.ndim)
    if grouped:
        shape = jax.ShapeDtypeStruct((channels // SUB, rows * SUB, LANES), jnp.bfloat16)
        out_spec = pl.BlockSpec((channels // SUB, block * SUB, LANES), lambda i: (0, i, 0))
    else:
        shape = jax.ShapeDtypeStruct((rows, channels, LANES), jnp.float32)
        out_spec = pl.BlockSpec((block, channels, LANES), lambda i: (i, 0, 0))
    return pl.pallas_call(
        functools.partial(encoder_kernel, grouped=grouped, dt=dt, per=per),
        grid=(rows // block,),
        out_shape=shape,
        in_specs=[pl.BlockSpec((slots, block, LANES), lambda i: (0, i, 0)),
                  pl.BlockSpec((block, LANES), lambda i: (i, 0)),
                  pl.BlockSpec((3, block, LANES), lambda i: (0, i, 0)),
                  whole(table), whole(first), whole(mid), whole(last)],
        out_specs=out_spec,
        scratch_shapes=[pltpu.VMEM((channels, block*LANES), jnp.float32)],
    )(codes, counts, centres, table, first, mid, last)

def pack_table(points):
    q = jnp.round(points * 32767.0).astype(jnp.int32)
    word = q[0::2] * 65536 + (q[1::2] + 32768)
    return word.reshape(3, -1, LANES)


def lane_maps(quarters, parts, inner_k, inner_j):
    grid = np.indices((quarters, 2, parts, inner_k, inner_j)).reshape(5, -1)
    return grid[0] * inner_j + grid[4], grid[2] * inner_k + grid[3], grid[1]


def spectral_tables(count_x, count_y, count_z, cells_x, cells_y, cells_z, group):
    keep = MODES
    signed = np.where(np.arange(keep) < keep // 2, np.arange(keep), np.arange(keep) - keep)
    mode_j, mode_k, imaginary = lane_maps(count_x, count_y, keep // count_y, keep // count_x)
    turn = 2.0 * np.pi / GRID
    rows_y = LANES // cells_z
    place_z, row_y, cell_z = np.indices((count_z, rows_y, cells_z)).reshape(3, -1)
    phase = turn * (
        (signed[mode_j] * row_y[:, None] + mode_k * (place_z * cells_z + cell_z)[:, None]) % GRID
    )
    forward = np.where(imaginary, -np.sin(phase), np.cos(phase))
    weight = np.where(mode_k == 0, 1.0, 2.0)
    inverse = (np.where(imaginary, -np.sin(phase), np.cos(phase)) * weight).T
    sign = np.where(imaginary, -1.0, 1.0)
    strip = turn * ((signed[mode_j] * (rows_y * np.arange(GRID // rows_y))[:, None]) % GRID)
    strips = np.stack([np.cos(strip), np.sin(strip) * sign])
    cell = np.arange(count_x * cells_x).reshape(count_x, 1, cells_x)
    angle = turn * ((signed[:, None] * cell) % GRID)
    eye = np.eye(group)

    def expand(values):
        wide = np.einsum("pab,cd->pacbd", values, eye)
        return wide.reshape(count_x, values.shape[1] * group, values.shape[2] * group)

    ahead = np.concatenate([expand(np.cos(angle)), expand(np.sin(angle))], axis=2)
    back = np.swapaxes(angle, 1, 2)
    back = np.concatenate([expand(np.cos(back)), expand(np.sin(back))], axis=2)
    partner = (keep - mode_j) % keep
    same = (
        (mode_j[:, None] == partner[None, :])
        & (mode_k[:, None] == 0)
        & (mode_k[None, :] == 0)
        & (imaginary[:, None] == imaginary[None, :])
        & (mode_j[:, None] != keep // 2)
    )
    flip = same * sign[None, :]
    power = np.where(mode_k == 0, 0.5, 2.0)
    lanes = np.stack([sign, power])
    narrow = lambda array: jnp.asarray(array.astype(np.float32), jnp.bfloat16)
    single = lambda array: jnp.asarray(array.astype(np.float32))
    return (
        narrow(forward),
        narrow(inverse),
        single(strips),
        narrow(ahead),
        narrow(back),
        narrow(flip),
        single(lanes),
    )


def swap_halves(values):
    return jnp.concatenate(
        [
            pltpu.roll(values[:, at : at + LANES], LANES // 2, 1)
            for at in range(0, values.shape[1], LANES)
        ],
        axis=1,
    )


def split(values):
    upper = values.astype(jnp.bfloat16)
    return upper, (values - upper.astype(jnp.float32)).astype(jnp.bfloat16)


def spectral_kernel(
    count_x,
    count_y,
    count_z,
    lat_ref,
    weight_ref,
    forward_ref,
    inverse_ref,
    strips_ref,
    ahead_ref,
    back_ref,
    flip_ref,
    lanes_ref,
    out_ref,
    came,
    plane,
    sums,
    sums_in,
    own,
    own_in,
    turned,
    mixed,
    mixed_in,
    joined,
    all_modes,
    pieces,
    send_a, recv_a, send_b, recv_b, send_c, recv_c, send_d, recv_d, send_e, recv_e, send_f, recv_f,
):
    place_x, place_y, place_z = lax.axis_index("gx"), lax.axis_index("gy"), lax.axis_index("gz")
    members = count_y * count_z
    me = place_y * count_z + place_z
    group = SUB
    strip_rows = plane.shape[0]
    half_modes = MODES // count_z
    inner = (MODES // count_x) * (MODES // count_y)
    mesh_id = pl.DeviceIdType.MESH

    def member(t):
        other = lax.rem(me + t, members)
        return other, {"gy": other // count_z, "gz": lax.rem(other, count_z)}

    def column(t):
        other = lax.rem(place_x + t, count_x)
        return other, {"gx": other}

    barrier = pltpu.get_barrier_semaphore()
    for t in range(1, members):
        pl.semaphore_signal(barrier, inc=1, device_id=member(t)[1], device_id_type=mesh_id)
    for t in range(1, count_x):
        pl.semaphore_signal(barrier, inc=1, device_id=column(t)[1], device_id_type=mesh_id)
    pl.semaphore_wait(barrier, members - 1 + count_x - 1)

    def exchange_with(peer, total, source, target, send, recv):
        copies = []
        for t in range(1, total):
            other, device = peer(t)
            copy = pltpu.make_async_remote_copy(
                src_ref=source(other),
                dst_ref=target,
                send_sem=send.at[t],
                recv_sem=recv.at[t],
                device_id=device,
                device_id_type=mesh_id,
            )
            copy.start()
            copies.append(copy)
        return copies

    copies = exchange_with(member, members, lambda p: lat_ref.at[p], came.at[me], send_a, recv_a)
    came[me] = lat_ref[me]
    sign = lanes_ref[0:1, :]
    plane[...] = jnp.zeros_like(plane)
    for copy in copies:
        copy.wait()

    strips = GRID // (came.shape[1] // strip_rows * count_y)
    chunks = came.shape[1] // strip_rows
    strips = chunks * count_y

    def ahead_step(strip, carry):
        source = strip // chunks
        at = pl.multiple_of(lax.rem(strip, chunks) * strip_rows, strip_rows)
        block = jnp.concatenate(
            [came[source * count_z + z, pl.ds(at, strip_rows), :] for z in range(count_z)], axis=1
        )
        part = jnp.dot(block, forward_ref[...], preferred_element_type=jnp.float32)
        cosine = strips_ref[0, pl.ds(strip, 1), :]
        sine = strips_ref[1, pl.ds(strip, 1), :]
        plane[...] += part * cosine + swap_halves(part) * sine
        return carry

    lax.fori_loop(0, strips, ahead_step, 0)
    whole = plane[...]
    whole_high, whole_low = split(whole)
    turn_high, turn_low = split(swap_halves(whole) * sign)
    table = ahead_ref[place_x]
    total = jnp.dot(
        table, jnp.concatenate([whole_high, turn_high], axis=0), preferred_element_type=jnp.float32
    ) + jnp.dot(
        table, jnp.concatenate([whole_low, turn_low], axis=0), preferred_element_type=jnp.float32
    )
    for q in range(count_x):
        sums[q] = total[:, LANES * q : LANES * (q + 1)]
    copies = exchange_with(column, count_x, lambda p: sums.at[p], sums_in.at[place_x], send_b, recv_b)
    sums_in[place_x] = sums[place_x]
    for copy in copies:
        copy.wait()
    spectrum = sums_in[0]
    for q in range(1, count_x):
        spectrum = spectrum + sums_in[q]
    half_rows = half_modes * group
    for z in range(count_z):
        own[z] = spectrum[half_rows * z : half_rows * (z + 1)].astype(jnp.bfloat16)

    copies = exchange_with(
        member, members, lambda p: own.at[lax.rem(p, count_z)], own_in.at[me], send_c, recv_c
    )
    own_in[me] = own[place_z]
    mixed_rows = lax.broadcasted_iota(jnp.int32, (2 * inner, LANES), 0) % inner
    mixed_lanes = lax.broadcasted_iota(jnp.int32, (2 * inner, LANES), 1) // (LANES // 2)
    modes_j = MODES // count_x
    modes_k = MODES // count_y
    row_mode = (mixed_rows % modes_j) * modes_k + mixed_rows // modes_j
    first_place = (place_x + place_y + place_z) == 0
    mode_zero = lax.broadcasted_iota(jnp.int32, (inner, LANES // 2), 0) == 0
    turned[...] = jnp.zeros_like(turned)
    for copy in copies:
        copy.wait()
    arrived = [own_in[p].astype(jnp.float32) for p in range(members)]
    for i in range(half_modes):
        column_values = jnp.concatenate([a[group * i : group * (i + 1)] for a in arrived], axis=0)
        column_values = jnp.concatenate([column_values, column_values], axis=0)
        mixed[i] = column_values.T
        at = pl.multiple_of(place_y * inner, inner)
        both = jnp.concatenate(
            [mixed[i, pl.ds(at, inner), :], mixed[i, pl.ds(LANES // 2 + at, inner), :]], axis=0
        )
        wide = jnp.concatenate(
            [
                jnp.where(row_mode == 2 * t + mixed_lanes, both, 0.0).astype(jnp.bfloat16)
                for t in range(inner // 2)
            ],
            axis=1,
        )
        by_real = jnp.dot(wide, weight_ref[0, i], preferred_element_type=jnp.float32)
        by_imag = jnp.dot(wide, weight_ref[1, i], preferred_element_type=jnp.float32)
        real = by_real[:inner] - by_imag[inner:]
        imag = by_imag[:inner] + by_real[inner:]
        if i == 0:
            drop = jnp.logical_and(mode_zero, first_place)
            real = jnp.where(drop, 0.0, real)
            imag = jnp.where(drop, 0.0, imag)
        turned[i, pl.ds(at, inner), 0 : LANES // 2] = real
        turned[i, pl.ds(LANES // 2 + at, inner), 0 : LANES // 2] = imag
    flat = [turned[i].T for i in range(half_modes)]
    for p in range(members):
        joined[p] = jnp.concatenate(
            [f[group * p : group * (p + 1)] for f in flat], axis=0
        ).astype(jnp.bfloat16)

    copies = exchange_with(member, members, lambda p: joined.at[p], mixed_in.at[me], send_d, recv_d)
    mixed_in[me] = joined[me]
    for copy in copies:
        copy.wait()
    parts = []
    for z in range(count_z):
        value = mixed_in[z].astype(jnp.float32)
        for y in range(1, count_y):
            value = value + mixed_in[y * count_z + z].astype(jnp.float32)
        parts.append(value)
    all_modes[place_x] = jnp.concatenate(parts, axis=0).astype(jnp.bfloat16)
    copies = exchange_with(
        column, count_x, lambda p: all_modes.at[place_x], all_modes.at[place_x], send_e, recv_e
    )
    for copy in copies:
        copy.wait()
    modes = jnp.concatenate([all_modes[q] for q in range(count_x)], axis=1)
    scaled = modes.astype(jnp.float32) * (1.0 / GRID**3)
    partner = jnp.dot(modes, flip_ref[...], preferred_element_type=jnp.float32) * (1.0 / GRID**3)
    energy = None
    for i in range(MODES):
        value = scaled[group * i : group * (i + 1)]
        term = value * value * lanes_ref[1:2, :]
        if i != MODES // 2:
            other = (MODES - i) % MODES
            term = term + 0.5 * value * partner[group * other : group * (other + 1)]
        energy = term if energy is None else energy + term
    variance = jnp.sum(energy, axis=1, keepdims=True)
    gain = 1.0 / jnp.sqrt(variance + NORM_FLOOR)
    rotated = (swap_halves(scaled * float(GRID**3)) * -sign).astype(jnp.bfloat16)
    back = jnp.dot(
        back_ref[place_x], jnp.concatenate([modes, rotated], axis=0), preferred_element_type=jnp.float32
    )
    back = back.reshape(-1, group, back.shape[1]) * (gain * (1.0 / GRID**3))[None]
    plane[...] = back.reshape(plane.shape)

    def back_step(strip, carry):
        source = strip // chunks
        at = pl.multiple_of(lax.rem(strip, chunks) * strip_rows, strip_rows)
        cosine = strips_ref[0, pl.ds(strip, 1), :]
        sine = strips_ref[1, pl.ds(strip, 1), :]
        value = plane[...]
        value = (value * cosine - swap_halves(value) * sine).astype(jnp.bfloat16)
        result = jnp.dot(value, inverse_ref[...], preferred_element_type=jnp.float32)
        for z in range(count_z):
            pieces[source * count_z + z, pl.ds(at, strip_rows), :] = result[
                :, LANES * z : LANES * (z + 1)
            ].astype(jnp.bfloat16)
        return carry

    lax.fori_loop(0, strips, back_step, 0)
    copies = exchange_with(member, members, lambda p: pieces.at[p], out_ref.at[me], send_f, recv_f)
    out_ref[me] = pieces[me]
    for copy in copies:
        copy.wait()


def spectral_branch(lat, spectral):
    count_x, count_y, count_z = (lax.axis_size(a) for a in ("gx", "gy", "gz"))
    members, piece_rows, _ = lat.shape
    cells_x, cells_y, cells_z = GRID // count_x, GRID // count_y, GRID // count_z
    strip_rows = cells_x * SUB
    half_modes = MODES // count_z
    channels = spectral.shape[-1]
    inner = (MODES // count_x) * (MODES // count_y)
    lanes = 2 * MODES * MODES
    tables = spectral_tables(count_x, count_y, count_z, cells_x, cells_y, cells_z, SUB)
    weight = spectral.reshape(2, half_modes, inner * channels, channels)
    vmem = lambda: pl.BlockSpec(memory_space=pltpu.VMEM)
    half = half_modes * SUB
    dma = pltpu.SemaphoreType.DMA
    return pl.pallas_call(
        functools.partial(spectral_kernel, count_x, count_y, count_z),
        out_shape=jax.ShapeDtypeStruct(lat.shape, jnp.bfloat16),
        in_specs=[vmem() for _ in range(9)],
        out_specs=vmem(),
        scratch_shapes=[
            pltpu.VMEM(lat.shape, jnp.bfloat16),
            pltpu.VMEM((strip_rows, lanes), jnp.float32),
            pltpu.VMEM((count_x, MODES * SUB, LANES), jnp.float32),
            pltpu.VMEM((count_x, MODES * SUB, LANES), jnp.float32),
            pltpu.VMEM((count_z, half, LANES), jnp.bfloat16),
            pltpu.VMEM((members, half, LANES), jnp.bfloat16),
            pltpu.VMEM((half_modes, LANES, LANES), jnp.float32),
            pltpu.VMEM((half_modes, LANES, LANES), jnp.float32),
            pltpu.VMEM((members, half, LANES), jnp.bfloat16),
            pltpu.VMEM((members, half, LANES), jnp.bfloat16),
            pltpu.VMEM((count_x, MODES * SUB, LANES), jnp.bfloat16),
            pltpu.VMEM(lat.shape, jnp.bfloat16),
        ]
        + [dma((members,))] * 2
        + [dma((count_x,))] * 2
        + [dma((members,))] * 2
        + [dma((members,))] * 2
        + [dma((count_x,))] * 2
        + [dma((members,))] * 2,
        compiler_params=pltpu.CompilerParams(
            collective_id=0, has_side_effects=True, vmem_limit_bytes=48 * 1024 * 1024
        ),
    )(lat, weight, *tables)


def final_kernel(branch_ref, lat_ref, skip_ref, out_ref):
    members, rows, _ = branch_ref.shape
    count = rows // SUB
    branch = [branch_ref[p].astype(jnp.float32) for p in range(members)]
    latent = [lat_ref[p].astype(jnp.float32) for p in range(members)]
    pick = lambda parts, x: jnp.concatenate([a[SUB * x : SUB * (x + 1)] for a in parts], axis=0)
    wide = jnp.concatenate([pick(latent, x) for x in range(count)], axis=1).astype(jnp.bfloat16)
    skip = jnp.dot(skip_ref[...], wide, preferred_element_type=jnp.float32)
    for x in range(count):
        v = pick(branch, x) + skip[:, LANES * x : LANES * (x + 1)]
        inner = v * (0.7978845608028654 + 0.035677408136300125 * (v * v))
        half = 0.5 * v
        out_ref[x, 0] = (half + half * jnp.tanh(inner)).T


def finish(branch, lat, skip_weight, cells_x):
    members, piece_rows, _ = lat.shape
    channels = skip_weight.shape[0]
    rows = cells_x * SUB
    piece = pl.BlockSpec((members, rows, LANES), lambda i: (0, i, 0))
    return pl.pallas_call(
        final_kernel,
        grid=(piece_rows // rows,),
        out_shape=jax.ShapeDtypeStruct((cells_x, piece_rows // rows, LANES, channels), jnp.float32),
        in_specs=[piece, piece, pl.BlockSpec(skip_weight.shape, lambda i: (0, 0))],
        out_specs=pl.BlockSpec((cells_x, 1, LANES, channels), lambda i: (0, i, 0, 0)),
    )(branch, lat, skip_weight.T)


def summed_over_axes(values, axes):
    for axis in axes:
        count = lax.axis_size(axis)
        copies = jnp.broadcast_to(values[None], (count,) + values.shape)
        values = jnp.sum(lax.all_to_all(copies, axis, 0, 0, tiled=True), axis=0)
    return values


def exchange(values, axis, split_axis, concat_axis):
    return lax.all_to_all(
        values.astype(jnp.bfloat16), axis, split_axis=split_axis, concat_axis=concat_axis, tiled=True
    ).astype(jnp.float32)


def body(point_data, neighbours, counts, kernel_in, kernel_mid, kernel_out, spectral, skip_weight):
    count_y = lax.axis_size("gy")
    count_z = lax.axis_size("gz")
    place_x = lax.axis_index("gx")
    place_y = lax.axis_index("gy")
    place_z = lax.axis_index("gz")
    geometry_count, cells_x, cells_y, cells_z = neighbours.shape[0:4]
    per_device = point_data.shape[2]
    channels = skip_weight.shape[0]
    cells = point_data[:, :, None, None, None]
    for dim, axis in enumerate(("gx", "gy", "gz")):
        cells = beside(cells, axis, dim + 2)
    table = cells.reshape(geometry_count, point_data.shape[1], -1)
    owner = neighbours // per_device
    offset_z, width_z = offset(owner % count_z, "gz")
    offset_y, width_y = offset(owner // count_z % count_y, "gy")
    offset_x, _ = offset(owner // (count_z * count_y), "gx")
    block_index = (offset_x * width_y + offset_y) * width_z + offset_z
    slot_index = neighbours % per_device
    centre_y = (
        (place_y * cells_y + jnp.arange(cells_y, dtype=jnp.int32)).astype(jnp.float32) + 0.5
    ) / GRID
    centre_z = (
        (place_z * cells_z + jnp.arange(cells_z, dtype=jnp.int32)).astype(jnp.float32) + 0.5
    ) / GRID
    centre_x = (
        (place_x * cells_x + jnp.arange(cells_x, dtype=jnp.int32)).astype(jnp.float32) + 0.5
    ) / GRID
    shape = (cells_x, cells_y, cells_z)
    rows_y = LANES // cells_z
    node_order = lambda values: jnp.swapaxes(
        values.reshape(values.shape[:-3] + (cells_x, cells_y // rows_y, LANES)), -3, -2
    ).reshape(values.shape[:-3] + (-1, LANES))
    centres = jnp.stack(
        [
            jnp.broadcast_to(centre_x[:, None, None], shape),
            jnp.broadcast_to(centre_y[None, :, None], shape),
            jnp.broadcast_to(centre_z[None, None, :], shape),
        ]
    )
    centres = node_order(centres / SCALE)
    code = block_index * per_device + slot_index
    grouped = (
        count_y * count_z * SUB == channels
        and cells_x * SUB == LANES
        and count_z * MODES // 2 == MODES
        and 2 * (MODES // lax.axis_size("gx")) * MODES == LANES
    )
    latent = []
    for geometry in range(geometry_count):
        turned = node_order(jnp.moveaxis(code[geometry], -1, 0))
        latent.append(
            encode(
                turned,
                node_order(counts[geometry]),
                centres,
                pack_table(table[geometry]),
                kernel_in,
                kernel_mid,
                kernel_out,
                grouped,
            )
        )
    if grouped:
        results = [
            finish(spectral_branch(lat, spectral), lat, skip_weight, cells_x) for lat in latent
        ]
        return jnp.stack(results).reshape(geometry_count, cells_x, cells_y, cells_z, channels)
    latent = jnp.swapaxes(jnp.stack(latent), 2, 3).astype(jnp.bfloat16)
    latent = latent.reshape(geometry_count, cells_y // rows_y, cells_x, LANES, channels)
    latent = jnp.swapaxes(latent, 1, 2)
    latent = latent.reshape(geometry_count, cells_x, cells_y, cells_z, channels)
    cos_centred, sin_centred = tables(GRID, MODES, True)
    cos_third, sin_third = tables(GRID, MODES, False)
    back_cos, back_sin = third_weights(cos_third, sin_third, GRID)
    depth_full = lax.all_to_all(latent, "gz", split_axis=4, concat_axis=3, tiled=True)
    real_part, imag_part = forward_real(
        depth_full.astype(jnp.float32), cos_third, sin_third, "gxyzc,kz->gxykc"
    )
    real_part, imag_part = (
        lax.all_to_all(real_part, "gy", split_axis=3, concat_axis=2, tiled=True),
        lax.all_to_all(imag_part, "gy", split_axis=3, concat_axis=2, tiled=True),
    )
    real_part, imag_part = forward_complex(
        real_part, imag_part, cos_centred, sin_centred, "gxykc,jy->gxjkc"
    )
    real_part, imag_part = (
        lax.all_to_all(real_part, "gx", split_axis=2, concat_axis=1, tiled=True),
        lax.all_to_all(imag_part, "gx", split_axis=2, concat_axis=1, tiled=True),
    )
    real_part, imag_part = forward_complex(
        real_part, imag_part, cos_centred, sin_centred, "gxjkc,ix->gijkc"
    )
    spec_real, spec_imag = (
        exchange(real_part, "gz", split_axis=1, concat_axis=4),
        exchange(imag_part, "gz", split_axis=1, concat_axis=4),
    )
    spec_real = spec_real.astype(jnp.bfloat16)
    spec_imag = spec_imag.astype(jnp.bfloat16)
    mixed_real = jnp.einsum(
        "gijkc,ijkco->gijko", spec_real, spectral[0], preferred_element_type=jnp.float32
    ) - jnp.einsum("gijkc,ijkco->gijko", spec_imag, spectral[1], preferred_element_type=jnp.float32)
    mixed_imag = jnp.einsum(
        "gijkc,ijkco->gijko", spec_real, spectral[1], preferred_element_type=jnp.float32
    ) + jnp.einsum("gijkc,ijkco->gijko", spec_imag, spectral[0], preferred_element_type=jnp.float32)
    first_place = (place_x + place_y + place_z) == 0
    modes = mixed_real.shape[1:4]
    order = sum(lax.broadcasted_iota(jnp.int32, modes, d) for d in range(3))
    zero_mode = ((order == 0) & first_place)[None, ..., None]
    mixed_real = jnp.where(zero_mode, 0.0, mixed_real)
    mixed_imag = jnp.where(zero_mode, 0.0, mixed_imag)
    mixed_real = mixed_real.astype(jnp.bfloat16)
    mixed_imag = mixed_imag.astype(jnp.bfloat16)
    real_part, imag_part = (
        exchange(mixed_real, "gz", split_axis=4, concat_axis=1),
        exchange(mixed_imag, "gz", split_axis=4, concat_axis=1),
    )
    real_part, imag_part = inverse_complex(
        real_part.astype(jnp.float32),
        imag_part.astype(jnp.float32),
        cos_centred,
        sin_centred,
        "gijkc,ix->gxjkc",
    )
    real_part, imag_part = (
        exchange(real_part, "gx", split_axis=1, concat_axis=2),
        exchange(imag_part, "gx", split_axis=1, concat_axis=2),
    )
    real_part, imag_part = inverse_complex(
        real_part, imag_part, cos_centred, sin_centred, "gxjkc,jy->gxykc"
    )
    real_part, imag_part = (
        exchange(real_part, "gy", split_axis=2, concat_axis=3),
        exchange(imag_part, "gy", split_axis=2, concat_axis=3),
    )
    depth_part = inverse_real(real_part, imag_part, back_cos, back_sin, "gxykc,kz->gxyzc")
    branch = exchange(depth_part, "gz", split_axis=3, concat_axis=4)
    skip = jnp.einsum("gxyzc,co->gxyzo", latent, skip_weight, preferred_element_type=jnp.float32)
    cells_total = float(GRID**3)
    variance = (
        summed_over_axes(jnp.sum(branch * branch, axis=(1, 2, 3)), ("gz", "gy", "gx")) / cells_total
    )
    normed = branch / jnp.sqrt(variance + NORM_FLOOR)[:, None, None, None, :]
    return jax.nn.gelu(normed + skip, approximate=True)


def solution(mesh):
    in_specs = (
        P(None, None, ("gx", "gy", "gz")),
        P(None, "gx", "gy", "gz", None),
        P(None, "gx", "gy", "gz"),
        P(),
        P(),
        P(),
        P(None, "gz", "gx", "gy", None, None),
        P(),
    )
    out_specs = P(None, "gx", "gy", "gz", None)
    return jax.shard_map(body, mesh=mesh, in_specs=in_specs, out_specs=out_specs, check_vma=False)
```

profile of v0, /device:TPU:0, one launch (start us, length us, event | category | flops | bytes accessed | tf_op | source)
XLA Modules:
  0.0 183.8 jit_solution(3814678325489140857)
XLA Ops:
  0.0 5.1 %collective-permute-start.1 = (f32[1,6,1,1,1,512]{5,0,4,3,2,1:T(1,128)}, f32[1,6,1,1,1,512]{5,0,4,3,2,1:T(1,128)S(1)}, u32[]{:S(2)}, u32[]{:S(2)}) collective-permute-start(f32[1,6,1,1,1,512]{5,0,4,3,2,1:T(1,128)} %bitcast.43), channel_id=1, source_target_pairs={{0,24},{8,0},{16,8},{24,16},{1,25},{9,1},{17,9},{25,17},{2,26},{10... | collective-permute-start | bytes 36872 | tf_op jit(solution)/shard_map/ppermute | solution.py:23
  5.1 0.7 convert_bitcast_fusion
  5.8 0.7 multiply_bitcast_fusion.1
  6.5 0.8 copy.23
  7.3 0.6 multiply_bitcast_fusion.mid_ref
  8.0 18.1 %fusion.9 = s32[1,16,16,32,32]{4,3,2,1,0:T(8,128)} fusion(s32[1,16,16,32,32]{4,3,2,1,0:T(8,128)} %param.16, s32[]{:T(128)S(6)} %axis_index.50, s32[]{:T(128)S(6)} %axis_index.48, s32[]{:T(128)S(6)} %axis_index.21), kind=kLoop, calls=%fused_computation.34 | loop fusion | flops 27000832 | bytes 2097164 | tf_op jit(solution)/shard_map/add | solution.py:610
  26.0 0.1 fusion.21
  26.2 0.1 stack_broadcast_in_dim.28
  26.3 0.1 stack_broadcast_in_dim.25
  26.5 0.7 collective-permute-start.3
  27.2 0.1 stack_broadcast_in_dim.23
  27.3 0.7 maximum_multiply_fusion.1
  27.9 0.7 copy.25
  28.6 0.1 reshape_squeeze.3
  28.7 0.6 copy.22
  29.3 0.1 convert_element_type.41
  29.5 0.8 copy.24.first_ref
  30.3 3.9 %copy.21 = s32[32,16,4,128]{3,1,2,0:T(8,128)} copy(s32[32,16,4,128]{0,3,2,1:T(8,128)} %bitcast.37) | data formatting | bytes 2097152 | tf_op jit(solution)/shard_map/reshape | solution.py:600
  34.2 0.1 pad_maximum_fusion
  34.3 1.6 collective-permute-start.4
  35.9 0.7 pad_maximum_fusion.2.last_ref
  36.5 3.7 %collective-permute-done.4 = f32[1,6,3,3,1,512]{5,0,4,3,2,1:T(1,128)S(1)} collective-permute-done((f32[1,6,3,3,1,512]{5,0,4,3,2,1:T(1,128)S(1)}, f32[1,6,3,3,1,512]{5,0,4,3,2,1:T(1,128)S(1)}, u32[]{:S(2)}, u32[]{:S(2)}) %collective-permute-start.4) | collective-permute-done | bytes 110624 | tf_op jit(solution)/shard_map/ppermute | solution.py:23
  40.2 0.8 fusion.20
  41.0 0.2 convert_element_type.38
  41.2 0.8 slice.7
  42.1 0.8 slice.6
  43.0 0.7 copy.28
  43.6 72.4 %shard_map.145.lat_ref = bf16[8,512,128]{2,1,0:T(8,128)(2,1)} custom-call(s32[32,64,128]{2,1,0:T(8,128)} %bitcast.39, s32[64,128]{1,0:T(8,128)} %bitcast.42, f32[3,64,128]{2,1,0:T(8,128)} %bitcast.41, s32[3,72,128]{2,1,0:T(8,128)} %bitcast.40, bf16[640,48]{1,0:T(8,128)(2,1)} %copy.24.first_ref, bf16[80,80]{1,0:T(8,128)(2,1)} %multiply_bitcast_fusion.mid_ref, ...), custom_call_target="tpu_custom_call" | custom-call | tf_op jit(solution)/shard_map/pallas_call | solution.py:175
  116.1 1.2 copy-done
  117.3 60.4 %shard_map.146.branch_ref = bf16[8,512,128]{2,1,0:T(8,128)(2,1)S(1)} custom-call(bf16[8,512,128]{2,1,0:T(8,128)(2,1)S(1)} %copy-done, bf16[2,8,1024,64]{3,2,1,0:T(8,128)(2,1)} %bitcast.38, bf16[256,512]{1,0:T(8,128)(2,1)S(1)} %copy-done.6, bf16[512,256]{1,0:T(8,128)(2,1)S(1)} %copy-done.5, f32[2,16,512]{2,1,0:T(8,128)S(1)} %copy-done.7, ...), custom_call_target="tpu_custom_call" | custom-call | tf_op jit(solution)/shard_map/pallas_call | solution.py:495
  177.8 1.0 copy-done.1
  178.7 5.0 %shard_map.147 = f32[16,4,128,64]{3,2,1,0:T(8,128)} custom-call(bf16[8,512,128]{2,1,0:T(8,128)(2,1)} %copy-done.1, bf16[8,512,128]{2,1,0:T(8,128)(2,1)} %shard_map.145.lat_ref, bf16[64,64]{1,0:T(8,128)(2,1)} %bitcast.48), custom_call_target="tpu_custom_call" | custom-call | tf_op jit(solution)/shard_map/pallas_call | solution.py:546
  (38 shorter events, 0.3 us)
Async XLA Ops:
  0.0 26.4 %collective-permute-start.1 = (f32[1,6,1,1,1,512]{5,0,4,3,2,1:T(1,128)}, f32[1,6,1,1,1,512]{5,0,4,3,2,1:T(1,128)S(1)}, u32[]{:S(2)}, u32[]{:S(2)}) collective-permute-start(f32[1,6,1,1,1,512]{5,0,4,3,2,1:T(1,128)} %bitcast.43), channel_id=1, source_target_pairs={{0,24},{8,0},{16,8},{24,16},{1,25},{9,1},{17,9},{25,17},{2,26},{10... | collective-permute-start | bytes 36872 | tf_op jit(solution)/shard_map/ppermute | solution.py:23
  5.1 21.3 %collective-permute-start = (f32[1,6,1,1,1,512]{5,0,4,3,2,1:T(1,128)}, f32[1,6,1,1,1,512]{5,0,4,3,2,1:T(1,128)S(1)}, u32[]{:S(2)}, u32[]{:S(2)}) collective-permute-start(f32[1,6,1,1,1,512]{5,0,4,3,2,1:T(1,128)} %bitcast.44), channel_id=1, source_target_pairs={{0,8},{8,16},{16,24},{24,0},{1,9},{9,17},{17,25},{25,1},{2,10},{10... | collective-permute-start | bytes 36872 | tf_op jit(solution)/shard_map/ppermute | solution.py:23
  8.0 18.5 %copy-start.10 = (f32[1,6,512]{2,0,1:T(1,128)S(1)}, f32[1,6,512]{2,0,1:T(1,128)}, u32[]{:S(2)}) copy-start(f32[1,6,512]{2,0,1:T(1,128)} %param.15) | copy-start | bytes 36868
  8.0 20.0 %copy-start.11 = (bf16[64,64]{1,0:T(8,128)(2,1)S(1)}, bf16[64,64]{1,0:T(8,128)(2,1)}, u32[]{:S(2)}) copy-start(bf16[64,64]{1,0:T(8,128)(2,1)} %param.22) | copy-start | bytes 24580
  8.0 20.7 %copy-start.9 = (s32[1,16,16,32]{3,2,1,0:T(8,128)S(1)}, s32[1,16,16,32]{3,2,1,0:T(8,128)}, u32[]{:S(2)}) copy-start(s32[1,16,16,32]{3,2,1,0:T(8,128)} %param.17) | copy-start | bytes 98308
  26.5 7.7 %collective-permute-start.3 = (f32[1,6,3,1,1,512]{5,0,4,3,2,1:T(1,128)S(1)}, f32[1,6,3,1,1,512]{5,0,4,3,2,1:T(1,128)S(1)}, u32[]{:S(2)}, u32[]{:S(2)}) collective-permute-start(f32[1,6,3,1,1,512]{5,0,4,3,2,1:T(1,128)S(1)} %pad_maximum_fusion.1), channel_id=1, source_target_pairs={{0,6},{2,0},{4,2},{6,4},{1,7},{3,1},{5,3},{7,5},{8,14},{10,8},{12,... | collective-permute-start | bytes 110600 | tf_op jit(solution)/shard_map/ppermute | solution.py:23
  27.2 7.0 %collective-permute-start.2 = (f32[1,6,3,1,1,512]{5,0,4,3,2,1:T(1,128)S(1)}, f32[1,6,3,1,1,512]{5,0,4,3,2,1:T(1,128)S(1)}, u32[]{:S(2)}, u32[]{:S(2)}) collective-permute-start(f32[1,6,3,1,1,512]{5,0,4,3,2,1:T(1,128)S(1)} %pad_maximum_fusion.1), channel_id=1, source_target_pairs={{0,2},{2,4},{4,6},{6,0},{1,3},{3,5},{5,7},{7,1},{8,10},{10,12},{12... | collective-permute-start | bytes 110600 | tf_op jit(solution)/shard_map/ppermute | solution.py:23
  30.3 85.8 %copy-start.2 = (bf16[512,512]{1,0:T(8,128)(2,1)S(1)}, bf16[512,512]{1,0:T(8,128)(2,1)}, u32[]{:S(2)}) copy-start(bf16[512,512]{1,0:T(8,128)(2,1)} %constant.142.clone.flip_ref) | copy-start | bytes 1572868
  30.3 85.8 %copy-start.3 = (bf16[4,128,256]{2,1,0:T(8,128)(2,1)S(1)}, bf16[4,128,256]{2,1,0:T(8,128)(2,1)}, u32[]{:S(2)}) copy-start(bf16[4,128,256]{2,1,0:T(8,128)(2,1)} %constant.141.clone.back_ref) | copy-start | bytes 786436
  30.3 85.8 %copy-start.4 = (bf16[4,128,256]{2,1,0:T(8,128)(2,1)S(1)}, bf16[4,128,256]{2,1,0:T(8,128)(2,1)}, u32[]{:S(2)}) copy-start(bf16[4,128,256]{2,1,0:T(8,128)(2,1)} %constant.140.clone.ahead_ref) | copy-start | bytes 786436
  30.3 85.8 %copy-start.5 = (bf16[512,256]{1,0:T(8,128)(2,1)S(1)}, bf16[512,256]{1,0:T(8,128)(2,1)}, u32[]{:S(2)}) copy-start(bf16[512,256]{1,0:T(8,128)(2,1)} %constant.138.clone.inverse_ref) | copy-start | bytes 786436
  30.3 85.8 %copy-start.6 = (bf16[256,512]{1,0:T(8,128)(2,1)S(1)}, bf16[256,512]{1,0:T(8,128)(2,1)}, u32[]{:S(2)}) copy-start(bf16[256,512]{1,0:T(8,128)(2,1)} %constant.137.clone.forward_ref) | copy-start | bytes 786436
  30.3 85.8 %copy-start.7 = (f32[2,16,512]{2,1,0:T(8,128)S(1)}, f32[2,16,512]{2,1,0:T(8,128)}, u32[]{:S(2)}) copy-start(f32[2,16,512]{2,1,0:T(8,128)} %constant.139.clone.strips_ref) | copy-start | bytes 196612
  30.3 85.8 %copy-start.8 = (f32[2,512]{1,0:T(2,128)S(1)}, f32[2,512]{1,0:T(2,128)}, u32[]{:S(2)}) copy-start(f32[2,512]{1,0:T(2,128)} %constant.143.clone.lanes_ref) | copy-start | bytes 12292
  34.3 5.9 %collective-permute-start.4 = (f32[1,6,3,3,1,512]{5,0,4,3,2,1:T(1,128)S(1)}, f32[1,6,3,3,1,512]{5,0,4,3,2,1:T(1,128)S(1)}, u32[]{:S(2)}, u32[]{:S(2)}) collective-permute-start(f32[1,6,3,3,1,512]{5,0,4,3,2,1:T(1,128)S(1)} %pad_maximum_fusion), channel_id=1, source_target_pairs={{0,1},{1,0},{2,3},{3,2},{4,5},{5,4},{6,7},{7,6},{8,9},{9,8},{10,11... | collective-permute-start | bytes 331784 | tf_op jit(solution)/shard_map/ppermute | solution.py:23
  116.1 1.2 copy-start
  177.7 1.0 copy-start.1
where the time goes:
time: 184 us
  Pallas kernels  138 us (75%)
  other arithmetic  22.5 us (12%)
  local copies, waits for them, and re-layouts  12.1 us (7%)
  starting transfers between devices  7.37 us (4%)
  waiting for transfers between devices  3.71 us (2%)
    pallas_call x1, Pallas kernels, encode(): pl.pallas_call(functools.partial(encoder_kernel, grouped=grouped, dt=dt,...  72.4 us
    pallas_call x1, Pallas kernels, spectral_branch(): pl.pallas_call(functools.partial(spectral_kernel, count_x, count_y, count...  60.4 us
    add x1, other arithmetic, body(): code = block_index * per_device + slot_index  18.1 us
    ppermute x5, starting transfers between devices, beside(): lax.ppermute(cells, axis, [(i, (i + by) % count) for i in range(count)])  7.37 us
    pallas_call x1, Pallas kernels, finish(): pl.pallas_call(final_kernel, grid=(piece_rows // rows,), out_shape=jax.Sh...  5.02 us
    unnamed x27, local copies, waits for them, and re-layouts  4.41 us
    reshape x1, local copies, waits for them, and re-layouts, body(): values.reshape(values.shape[:-3] + (cells_x, cells_y // rows_y, LANES))  3.86 us
    ppermute x5, waiting for transfers between devices, beside(): lax.ppermute(cells, axis, [(i, (i + by) % count) for i in range(count)])  3.71 us
  transfers between devices with their start and end apart: 5, of which 1 were waited for; matrix products, arithmetic and copies ran while one was open for 16% of the time, Pallas kernels for 0%

commit v1 on v0

--- a/solution.py
+++ b/solution.py
@@ -16,21 +16,6 @@
 
 HIGH = lax.Precision.HIGH
 NORM_FLOOR = 1.0
-
-
-def beside(cells, axis, dim):
-    count = lax.axis_size(axis)
-    turn = lambda by: lax.ppermute(cells, axis, [(i, (i + by) % count) for i in range(count)])
-    if count == 1:
-        return cells
-    if count == 2:
-        return jnp.concatenate([cells, turn(1)], axis=dim)
-    return jnp.concatenate([turn(1), cells, turn(-1)], axis=dim)
-
-
-def offset(owner, axis):
-    count = lax.axis_size(axis)
-    return (owner - lax.axis_index(axis) + (1 if count > 2 else 0)) % count, min(count, 3)
 
 
 def tables(length, keep_count, centred):
@@ -79,12 +64,15 @@
 
 SUB = 8
 LANES = 128
-
 SCALE = 0.035677408136300125 ** (-1.0 / 3.0)
 SHIFT = 0.7978845608028654 * SCALE
-
-def gelu2(y):
+FINE = 1023.0
+COARSE = 511.0
+
+
+def double_gelu(y):
     return y + y * jnp.tanh(y * (y * y + jnp.asarray(SHIFT, y.dtype)))
+
 
 def pick(leaf, bits, low, high, level):
     if high - low == 1:
@@ -92,102 +80,254 @@
     half = 1 << (level - 1)
     if low + half >= high:
         return pick(leaf, bits, low, high, level - 1)
-    a = pick(leaf, bits, low, low + half, level - 1)
-    b = pick(leaf, bits, low + half, high, level - 1)
-    return jnp.where(bits[level - 1], b, a)
-
-def encoder_kernel(codes_ref, counts_ref, centres_ref, table_ref, first_ref, mid_ref, last_ref, out_ref, acc_ref, grouped, dt=jnp.bfloat16, per=2):
-    slots, rows = codes_ref.shape[0:2]
-    groups = rows // SUB
-    words, table_rows = table_ref.shape[0:2]
+    first = pick(leaf, bits, low, low + half, level - 1)
+    second = pick(leaf, bits, low + half, high, level - 1)
+    return jnp.where(bits[level - 1], second, first)
+
+
+def over(values, count):
+    return values >> (count.bit_length() - 1) if count & (count - 1) == 0 else values // count
+
+
+def within(values, count):
+    return values & (count - 1) if count & (count - 1) == 0 else lax.rem(values, count)
+
+
+def offset(owner, place, count):
+    return within(owner - place + (count + (1 if count > 2 else 0)), count)
+
+
+def encoder_kernel(
+    sizes, grouped, neighbours_ref, counts_ref, table_ref, in_ref, mid_ref, last_ref, out_ref,
+    codes, first, middle, final, stack, one, two, total,
+):
+    count_x, count_y, count_z, per_device = sizes
+    place_x, place_y, place_z = lax.axis_index("gx"), lax.axis_index("gy"), lax.axis_index("gz")
+    cells_x, cells_y, cells_z, slots = neighbours_ref.shape
+    rows_y = LANES // cells_z
+    rows = counts_ref.shape[0]
     units = mid_ref.shape[0]
-    channels = last_ref.shape[0]
+    channels = last_ref.shape[1]
+    words, table_rows = in_ref.shape[0] // 3, table_ref.shape[0]
     depth = max(1, (table_rows - 1).bit_length())
-    acc_ref[...] = jnp.zeros_like(acc_ref)
-    counts = [counts_ref[SUB*g:SUB*(g+1), :] for g in range(groups)]
-    scale = 1.0 / (32767.0 * SCALE)
-    def pairs(i):
-        out = []
+    per = stack.shape[0]
+    block = total.shape[2] // LANES
+    groups = block // SUB
+    turns = slots // per
+    blocks = rows // block
+
+    iota = lambda shape, d: lax.broadcasted_iota(jnp.int32, shape, d)
+    spread = jnp.where(iota((SUB * units, units), 0) % units == iota((SUB * units, units), 1), 1.0, 0.0)
+    values = 3 * words
+    wide = jnp.where(iota((values, values * SUB), 0) == iota((values, values * SUB), 1) // SUB, 1.0, 0.0)
+    narrow = lambda a: a.astype(jnp.bfloat16)
+    inputs = in_ref[...].astype(jnp.float32).T
+    tiled = jnp.dot(narrow(inputs), narrow(wide), preferred_element_type=jnp.float32)
+    tiled = jnp.dot(narrow(spread), narrow(tiled), preferred_element_type=jnp.float32)
+    shape = (SUB * units, values * SUB)
+    first[...] = narrow(jnp.where(iota(shape, 0) // units == iota(shape, 1) % SUB, tiled, 0.0))
+    middle[...] = narrow(mid_ref[...].astype(jnp.float32).T * 0.5)
+    turned = narrow(last_ref[...].astype(jnp.float32).T * 0.5)
+    for k in range(per):
+        final[:, units * k : units * (k + 1)] = turned
+    one[...] = jnp.zeros_like(one)
+    two[...] = jnp.zeros_like(two)
+    total[...] = jnp.zeros_like(total)
+    width_y, width_z = min(count_y, 3), min(count_z, 3)
+
+    def prepare(row, carry):
+        strip, x = row // cells_x, lax.rem(row, cells_x)
+        near = neighbours_ref[x, pl.ds(strip * rows_y, rows_y)].reshape(LANES, slots).T
+        owner = over(near, per_device)
+        at_z = offset(within(owner, count_z), place_z, count_z)
+        at_y = offset(within(over(owner, count_z), count_y), place_y, count_y)
+        at_x = offset(over(owner, count_z * count_y), place_x, count_x)
+        code = ((at_x * width_y + at_y) * width_z + at_z) * per_device + within(near, per_device)
+        codes[pl.ds(pl.multiple_of(row * slots, SUB), slots), :] = code
+        return carry
+
+    lax.fori_loop(0, rows, prepare, 0, unroll=min(8, rows))
+    lane_ids = iota((SUB, LANES), 1)
+    sub_ids = iota((SUB, LANES), 0)
+    centre = lambda cell: (cell.astype(jnp.float32) + 0.5) * (1.0 / (GRID * SCALE))
+    centre_z = centre(place_z * cells_z + within(lane_ids, cells_z))
+    centre_x = [
+        centre(place_x * cells_x + within(SUB * g + sub_ids, cells_x)) for g in range(groups)
+    ]
+    lane_y = over(lane_ids, cells_z) + place_y * cells_y
+
+    def pairs(t):
+        here = jnp.minimum(t // turns, blocks - 1)
+        turn = lax.rem(t, turns)
+        limit = jnp.where(t < blocks * turns, 0, slots)
+        centre_y = centre(lane_y + (here * block // cells_x) * rows_y)
         for k in range(per):
-            s = i * per + k
-            stacks = []
+            slot = turn * per + k
             for g in range(groups):
-                code = codes_ref[s, SUB*g:SUB*(g+1), :]
+                base = here * block + SUB * g
+                code = codes[pl.ds(base * slots + slot, SUB, stride=slots), :]
                 lane = code & (LANES - 1)
                 bits = [(code & (LANES << b)) != 0 for b in range(depth)]
-                live = s < counts[g]
-                vals = []
+                live = slot + limit < counts_ref[pl.ds(pl.multiple_of(base, SUB), SUB), :]
+                found = []
                 for w in range(words):
                     leaf = lambda r: jnp.take_along_axis(
-                        jnp.broadcast_to(table_ref[w, r:r+1, :], (SUB, LANES)), lane, axis=1, mode="promise_in_bounds")
+                        jnp.broadcast_to(table_ref[r, 3 * w : 3 * w + 1, :], (SUB, LANES)),
+                        lane,
+                        axis=1,
+                        mode="promise_in_bounds",
+                    )
                     word = pick(leaf, bits, 0, table_rows, depth)
-                    vals += [word >> 16, (word & 65535) - 32768]
+                    found += [word >> 21, ((word >> 10) & 2047) - 1024, (word & 1023) - 512]
                 parts = []
-                for v in range(6):
-                    x = vals[v].astype(jnp.float32) * scale
+                for v, x in enumerate(found):
+                    x = x.astype(jnp.float32) * (1.0 / (SCALE * (COARSE if v % 3 == 2 else FINE)))
                     if v < 3:
-                        x = x - centres_ref[v, SUB*g:SUB*(g+1), :]
+                        x = x - (centre_x[g], centre_y, centre_z)[v]
                     parts.append(jnp.where(live, x, 0.0))
-                stacks.append(jnp.concatenate(parts, axis=0).astype(jnp.bfloat16))
-            out.append(jnp.concatenate(stacks, axis=1))
-        return out
-    def step(i, stacks):
-        h2s = []
+                stack[k, :, LANES * g : LANES * (g + 1)] = narrow(jnp.concatenate(parts, axis=0))
+
+    def step(t, carry):
+        there = jnp.maximum(t - 2, 0) // turns
+        total[there] += jnp.dot(final[...], two[...], preferred_element_type=jnp.float32)
         for k in range(per):
-            z1 = jnp.dot(first_ref[...], stacks[k], preferred_element_type=jnp.float32)
-            h1 = gelu2(z1.astype(dt)).astype(jnp.bfloat16)
-            wide = jnp.concatenate([h1[units*r:units*(r+1)] for r in range(SUB)], axis=1)
-            z2 = jnp.dot(mid_ref[...], wide, preferred_element_type=jnp.float32)
-            h2s.append(gelu2(z2.astype(dt)).astype(jnp.bfloat16))
-        hidden = jnp.concatenate(h2s, axis=0)
-        acc_ref[...] += jnp.dot(last_ref[...], hidden, preferred_element_type=jnp.float32)
-        return pairs(jnp.minimum(i + 1, slots // per - 1))
-    lax.fori_loop(0, slots // per, step, pairs(0))
-    done = {}
-    for r in range(SUB):
-        for g in range(groups):
-            at = (r * groups + g) * LANES
-            row = SUB * g + r
-            done[row] = acc_ref[:, at:at+LANES] * SCALE / counts_ref[row:row+1, :].astype(jnp.float32)
-            if not grouped:
-                out_ref[row] = done[row]
-    if grouped:
-        for q in range(channels // SUB):
-            out_ref[q] = jnp.concatenate(
-                [done[row][SUB * q : SUB * (q + 1)] for row in range(rows)], axis=0
-            ).astype(jnp.bfloat16)
-
-def encode(codes, counts, centres, table, kernel_in, kernel_mid, kernel_out, grouped, dt=jnp.bfloat16, per=2):
-    slots, rows = codes.shape[0:2]
+            z = jnp.dot(middle[...], one[k], preferred_element_type=jnp.float32)
+            two[units * k : units * (k + 1), :] = double_gelu(narrow(z))
+        for k in range(per):
+            z = jnp.dot(first[...], stack[k], preferred_element_type=jnp.float32)
+            h = double_gelu(narrow(z))
+            for r in range(SUB):
+                at = r * groups * LANES
+                one[k, :, at : at + groups * LANES] = h[units * r : units * (r + 1)]
+        pairs(t + 1)
+        return carry
+
+    pairs(0)
+    lax.fori_loop(0, blocks * turns + 2, step, 0)
+
+    def close(b, carry):
+        done = {}
+        for r in range(SUB):
+            for g in range(groups):
+                at = (r * groups + g) * LANES
+                row = SUB * g + r
+                count = counts_ref[pl.ds(b * block + row, 1), :].astype(jnp.float32)
+                done[row] = total[b, :, at : at + LANES] * (SCALE / count)
+                if not grouped:
+                    out_ref[b * block + row] = done[row]
+        if grouped:
+            for q in range(channels // SUB):
+                out_ref[q, pl.ds(pl.multiple_of(b * block * SUB, SUB * SUB), block * SUB), :] = narrow(
+                    jnp.concatenate(
+                        [done[row][SUB * q : SUB * (q + 1)] for row in range(block)], axis=0
+                    )
+                )
+        return carry
+
+    lax.fori_loop(0, blocks, close, 0)
+
+
+def encode(neighbours, counts, table, kernel_in, kernel_mid, kernel_out, per_device, grouped):
+    rows = counts.shape[0]
+    slots = neighbours.shape[-1]
     units, channels = kernel_out.shape
-    block = min(16, rows)
-    w1 = kernel_in.T.astype(jnp.float32)
-    first = jnp.einsum("hv,rq->rhvq", w1, jnp.eye(SUB, dtype=jnp.float32)).reshape(SUB*units, 6*SUB).astype(jnp.bfloat16)
-    mid = (kernel_mid.T * 0.5).astype(jnp.bfloat16)
-    last = jnp.concatenate([(kernel_out.T * 0.5).astype(jnp.bfloat16)]*per, axis=1)
-    whole = lambda a: pl.BlockSpec(a.shape, lambda i: (0,)*a.ndim)
+    block = min(2 * SUB, rows)
+    per = 2
     if grouped:
         shape = jax.ShapeDtypeStruct((channels // SUB, rows * SUB, LANES), jnp.bfloat16)
-        out_spec = pl.BlockSpec((channels // SUB, block * SUB, LANES), lambda i: (0, i, 0))
     else:
         shape = jax.ShapeDtypeStruct((rows, channels, LANES), jnp.float32)
-        out_spec = pl.BlockSpec((block, channels, LANES), lambda i: (i, 0, 0))
+    sizes = tuple(lax.axis_size(a) for a in ("gx", "gy", "gz")) + (per_device,)
+    vmem = lambda: pl.BlockSpec(memory_space=pltpu.VMEM)
+    values = kernel_in.shape[0]
     return pl.pallas_call(
-        functools.partial(encoder_kernel, grouped=grouped, dt=dt, per=per),
-        grid=(rows // block,),
+        functools.partial(encoder_kernel, sizes, grouped),
         out_shape=shape,
-        in_specs=[pl.BlockSpec((slots, block, LANES), lambda i: (0, i, 0)),
-                  pl.BlockSpec((block, LANES), lambda i: (i, 0)),
-                  pl.BlockSpec((3, block, LANES), lambda i: (0, i, 0)),
-                  whole(table), whole(first), whole(mid), whole(last)],
-        out_specs=out_spec,
-        scratch_shapes=[pltpu.VMEM((channels, block*LANES), jnp.float32)],
-    )(codes, counts, centres, table, first, mid, last)
-
-def pack_table(points):
-    q = jnp.round(points * 32767.0).astype(jnp.int32)
-    word = q[0::2] * 65536 + (q[1::2] + 32768)
-    return word.reshape(3, -1, LANES)
+        in_specs=[vmem() for _ in range(6)],
+        out_specs=vmem(),
+        scratch_shapes=[
+            pltpu.VMEM((rows * slots, LANES), jnp.int32),
+            pltpu.VMEM((SUB * units, values * SUB), jnp.bfloat16),
+            pltpu.VMEM((units, units), jnp.bfloat16),
+            pltpu.VMEM((channels, per * units), jnp.bfloat16),
+            pltpu.VMEM((per, values * SUB, block // SUB * LANES), jnp.bfloat16),
+            pltpu.VMEM((per, units, block * LANES), jnp.bfloat16),
+            pltpu.VMEM((per * units, block * LANES), jnp.bfloat16),
+            pltpu.VMEM((rows // block, channels, block * LANES), jnp.float32),
+        ],
+        compiler_params=pltpu.CompilerParams(vmem_limit_bytes=40 * 1024 * 1024),
+    )(neighbours, counts, table, kernel_in, kernel_mid, kernel_out)
+
+
+def halo_kernel(sizes, points_ref, out_ref, near, send, recv):
+    places = [lax.axis_index(a) for a in ("gx", "gy", "gz")]
+    widths = [min(n, 3) for n in sizes]
+    home = [1 if n > 2 else 0 for n in sizes]
+    blocks = [
+        (x, y, z) for x in range(widths[0]) for y in range(widths[1]) for z in range(widths[2])
+    ]
+    number = lambda b: (b[0] * widths[1] + b[1]) * widths[2] + b[2]
+
+    def reader(block):
+        there = [lax.rem(p - o + h + n, n) for p, o, h, n in zip(places, block, home, sizes)]
+        return dict(zip(("gx", "gy", "gz"), there))
+
+    others = [b for b in blocks if list(b) != home]
+    barrier = pltpu.get_barrier_semaphore()
+    for block in others:
+        pl.semaphore_signal(
+            barrier, inc=1, device_id=reader(block), device_id_type=pl.DeviceIdType.MESH
+        )
+    pl.semaphore_wait(barrier, len(others))
+    copies = {}
+    for block in others:
+        b = number(block)
+        copies[b] = pltpu.make_async_remote_copy(
+            src_ref=points_ref,
+            dst_ref=near.at[b],
+            send_sem=send.at[b],
+            recv_sem=recv.at[b],
+            device_id=reader(block),
+            device_id_type=pl.DeviceIdType.MESH,
+        )
+        copies[b].start()
+    pieces = points_ref.shape[1] // LANES
+    for block in [tuple(home)] + others:
+        b = number(block)
+        if b in copies:
+            copies[b].wait()
+            values = near[b]
+        else:
+            values = points_ref[...]
+        values = jnp.concatenate([values, values[0 : SUB - values.shape[0]]], axis=0)
+        fine = jnp.round(values * FINE).astype(jnp.int32)
+        coarse = jnp.round(values * COARSE).astype(jnp.int32)
+        for r in range(pieces):
+            part = fine[:, LANES * r : LANES * (r + 1)]
+            third = coarse[:, LANES * r : LANES * (r + 1)]
+            out_ref[b * pieces + r] = (
+                part * 2097152
+                + (pltpu.roll(part, SUB - 1, 0) + 1024) * 1024
+                + (pltpu.roll(third, SUB - 2, 0) + 512)
+            )
+
+
+def point_table(points):
+    sizes = tuple(lax.axis_size(a) for a in ("gx", "gy", "gz"))
+    blocks = math.prod(min(n, 3) for n in sizes)
+    vmem = pl.BlockSpec(memory_space=pltpu.VMEM)
+    return pl.pallas_call(
+        functools.partial(halo_kernel, sizes),
+        out_shape=jax.ShapeDtypeStruct((blocks * points.shape[1] // LANES, SUB, LANES), jnp.int32),
+        in_specs=[vmem],
+        out_specs=vmem,
+        scratch_shapes=[
+            pltpu.VMEM((blocks,) + points.shape, jnp.float32),
+            pltpu.SemaphoreType.DMA((blocks,)),
+            pltpu.SemaphoreType.DMA((blocks,)),
+        ],
+        compiler_params=pltpu.CompilerParams(collective_id=1, has_side_effects=True),
+    )(points)
 
 
 def lane_maps(quarters, parts, inner_k, inner_j):
@@ -329,20 +469,36 @@
             copies.append(copy)
         return copies
 
-    copies = exchange_with(member, members, lambda p: lat_ref.at[p], came.at[me], send_a, recv_a)
+    def apart(d, e):
+        other = {
+            "gy": lax.rem(place_y + count_y - d, count_y),
+            "gz": lax.rem(place_z + e, count_z),
+        }
+        return other["gy"] * count_z + other["gz"], other
+
+    def send_to(d, e, source, target, send, recv):
+        other, device = apart(d, e)
+        copy = pltpu.make_async_remote_copy(
+            src_ref=source.at[other],
+            dst_ref=target.at[me],
+            send_sem=send.at[d * count_z + e],
+            recv_sem=recv.at[d * count_z + e],
+            device_id=device,
+            device_id_type=mesh_id,
+        )
+        copy.start()
+        return copy
+
+    steps = [(d, e) for d in range(count_y) for e in range(count_z)]
+    arrivals = {s: send_to(*s, lat_ref, came, send_a, recv_a) for s in steps if s != (0, 0)}
     came[me] = lat_ref[me]
     sign = lanes_ref[0:1, :]
     plane[...] = jnp.zeros_like(plane)
-    for copy in copies:
-        copy.wait()
-
-    strips = GRID // (came.shape[1] // strip_rows * count_y)
     chunks = came.shape[1] // strip_rows
-    strips = chunks * count_y
-
-    def ahead_step(strip, carry):
-        source = strip // chunks
-        at = pl.multiple_of(lax.rem(strip, chunks) * strip_rows, strip_rows)
+
+    def ahead_step(source, chunk, carry):
+        strip = source * chunks + chunk
+        at = pl.multiple_of(chunk * strip_rows, strip_rows)
         block = jnp.concatenate(
             [came[source * count_z + z, pl.ds(at, strip_rows), :] for z in range(count_z)], axis=1
         )
@@ -352,7 +508,12 @@
         plane[...] += part * cosine + swap_halves(part) * sine
         return carry
 
-    lax.fori_loop(0, strips, ahead_step, 0)
+    for d in range(count_y):
+        for e in range(count_z):
+            if (d, e) in arrivals:
+                arrivals[d, e].wait()
+        source = lax.rem(place_y + d, count_y)
+        lax.fori_loop(0, chunks, functools.partial(ahead_step, source), 0)
     whole = plane[...]
     whole_high, whole_low = split(whole)
     turn_high, turn_low = split(swap_halves(whole) * sign)
@@ -457,9 +618,9 @@
     back = back.reshape(-1, group, back.shape[1]) * (gain * (1.0 / GRID**3))[None]
     plane[...] = back.reshape(plane.shape)
 
-    def back_step(strip, carry):
-        source = strip // chunks
-        at = pl.multiple_of(lax.rem(strip, chunks) * strip_rows, strip_rows)
+    def back_step(source, chunk, carry):
+        strip = source * chunks + chunk
+        at = pl.multiple_of(chunk * strip_rows, strip_rows)
         cosine = strips_ref[0, pl.ds(strip, 1), :]
         sine = strips_ref[1, pl.ds(strip, 1), :]
         value = plane[...]
@@ -471,8 +632,13 @@
             ].astype(jnp.bfloat16)
         return carry
 
-    lax.fori_loop(0, strips, back_step, 0)
-    copies = exchange_with(member, members, lambda p: pieces.at[p], out_ref.at[me], send_f, recv_f)
+    copies = []
+    for d in [*range(1, count_y), 0]:
+        source = lax.rem(place_y + count_y - d, count_y)
+        lax.fori_loop(0, chunks, functools.partial(back_step, source), 0)
+        copies += [
+            send_to(d, e, pieces, out_ref, send_f, recv_f) for e in range(count_z) if (d, e) != (0, 0)
+        ]
     out_ref[me] = pieces[me]
     for copy in copies:
         copy.wait()
@@ -575,39 +741,10 @@
     geometry_count, cells_x, cells_y, cells_z = neighbours.shape[0:4]
     per_device = point_data.shape[2]
     channels = skip_weight.shape[0]
-    cells = point_data[:, :, None, None, None]
-    for dim, axis in enumerate(("gx", "gy", "gz")):
-        cells = beside(cells, axis, dim + 2)
-    table = cells.reshape(geometry_count, point_data.shape[1], -1)
-    owner = neighbours // per_device
-    offset_z, width_z = offset(owner % count_z, "gz")
-    offset_y, width_y = offset(owner // count_z % count_y, "gy")
-    offset_x, _ = offset(owner // (count_z * count_y), "gx")
-    block_index = (offset_x * width_y + offset_y) * width_z + offset_z
-    slot_index = neighbours % per_device
-    centre_y = (
-        (place_y * cells_y + jnp.arange(cells_y, dtype=jnp.int32)).astype(jnp.float32) + 0.5
-    ) / GRID
-    centre_z = (
-        (place_z * cells_z + jnp.arange(cells_z, dtype=jnp.int32)).astype(jnp.float32) + 0.5
-    ) / GRID
-    centre_x = (
-        (place_x * cells_x + jnp.arange(cells_x, dtype=jnp.int32)).astype(jnp.float32) + 0.5
-    ) / GRID
-    shape = (cells_x, cells_y, cells_z)
     rows_y = LANES // cells_z
     node_order = lambda values: jnp.swapaxes(
-        values.reshape(values.shape[:-3] + (cells_x, cells_y // rows_y, LANES)), -3, -2
-    ).reshape(values.shape[:-3] + (-1, LANES))
-    centres = jnp.stack(
-        [
-            jnp.broadcast_to(centre_x[:, None, None], shape),
-            jnp.broadcast_to(centre_y[None, :, None], shape),
-            jnp.broadcast_to(centre_z[None, None, :], shape),
-        ]
-    )
-    centres = node_order(centres / SCALE)
-    code = block_index * per_device + slot_index
+        values.reshape(cells_x, cells_y // rows_y, LANES), 0, 1
+    ).reshape(-1, LANES)
     grouped = (
         count_y * count_z * SUB == channels
         and cells_x * SUB == LANES
@@ -616,16 +753,15 @@
     )
     latent = []
     for geometry in range(geometry_count):
-        turned = node_order(jnp.moveaxis(code[geometry], -1, 0))
         latent.append(
             encode(
-                turned,
+                neighbours[geometry],
                 node_order(counts[geometry]),
-                centres,
-                pack_table(table[geometry]),
+                point_table(point_data[geometry]),
                 kernel_in,
                 kernel_mid,
                 kernel_out,
+                per_device,
                 grouped,
             )
         )

time: 184 us -> 141 us (0.77)
  other arithmetic: 22.5 us -> 0 us
  Pallas kernels: 138 us -> 130 us
  starting transfers between devices: 7.37 us -> 0 us
  waiting for transfers between devices: 3.71 us -> 0 us
  local copies, waits for them, and re-layouts: 12.1 us -> 10.1 us
    add x1 -> x0, other arithmetic: 18.1 us -> none  [body(): code = block_index * per_device + slot_index]
    ppermute x5 -> x0, starting transfers between devices: 7.37 us -> none  [beside(): lax.ppermute(cells, axis, [(i, (i + by) % count) for i in range(count)])]
    unnamed x27 -> x29, local copies, waits for them, and re-layouts: 4.41 us -> 9.13 us
    pallas_call x1, Pallas kernels: 60.4 us -> 56.4 us  [spectral_branch(): pl.pallas_call(functools.partial(spectral_kernel, count_x, count_y, count...]
    reshape x1 -> x0, local copies, waits for them, and re-layouts: 3.86 us -> none  [body(): values.reshape(values.shape[:-3] + (cells_x, cells_y // rows_y, LANES))]
    pallas_call x1 -> x2, Pallas kernels: 72.4 us -> 68.6 us  [the longest x1 55.2 us: encode(): pl.pallas_call(functools.partial(encoder_kernel, sizes, grouped), out_sha...]
    ppermute x5 -> x0, waiting for transfers between devices: 3.71 us -> none  [beside(): lax.ppermute(cells, axis, [(i, (i + by) % count) for i in range(count)])]
  transfers between devices with their start and end apart: 5 -> 0, of which waited for: 1 -> 0; matrix products, arithmetic and copies ran while one was open for 16% -> 0% of each run, Pallas kernels for 0% -> 0%
where the time goes in v1:
time: 141 us; the launch traced here: 140 us
  Pallas kernels  130 us (92%)
  local copies, waits for them, and re-layouts  10.1 us (7%)
    pallas_call x1, Pallas kernels, spectral_branch(): pl.pallas_call(functools.partial(spectral_kernel, count_x, count_y, count...  56.4 us
    pallas_call x1, Pallas kernels, encode(): pl.pallas_call(functools.partial(encoder_kernel, sizes, grouped), out_sha...  55.2 us
    pallas_call x1, Pallas kernels, point_table(): pl.pallas_call(functools.partial(halo_kernel, sizes), out_shape=jax.Shape...  13.5 us
    unnamed x29, local copies, waits for them, and re-layouts  9.13 us
    pallas_call x1, Pallas kernels, finish(): pl.pallas_call(final_kernel, grid=(piece_rows // rows,), out_shape=jax.Sh...  5.02 us

profile of v1, /device:TPU:0, one launch (start us, length us, event | category | flops | bytes accessed | tf_op | source)
XLA Modules:
  0.0 140.3 jit_solution(11953495950475454114)
XLA Ops:
  0.0 0.0 copy-start.11
  0.0 0.0 copy-start.4
  0.0 1.4 copy.21
  1.4 1.4 copy.18
  2.8 0.8 copy.17.last_ref
  3.6 1.0 reshape_squeeze.3
  4.6 13.5 %shard_map.145.table_ref = s32[72,8,128]{2,1,0:T(8,128)} custom-call(f32[6,512]{1,0:T(8,128)} %bitcast.16), custom_call_target="tpu_custom_call" | custom-call | tf_op jit(solution)/shard_map/pallas_call | solution.py:319
  18.1 0.0 copy-start.1
  18.1 2.2 %copy-done.1 = s32[1,16,16,32,32]{4,3,2,1,0:T(8,128)S(1)} copy-done((s32[1,16,16,32,32]{4,3,2,1,0:T(8,128)S(1)}, s32[1,16,16,32,32]{4,3,2,1,0:T(8,128)}, u32[]{:S(2)}) %copy-start.1) | copy-done | bytes 1048600
  20.3 0.0 copy-start.3
  20.3 1.0 copy-done.3
  21.3 0.0 copy-start.10
  21.3 0.7 copy-done.10
  22.0 0.0 copy-start.12
  22.0 0.7 copy-done.12
  22.7 0.0 copy-start.5
  22.7 0.0 copy-start.6
  22.7 0.0 copy-start.7
  22.7 55.2 %shard_map.146.lat_ref = bf16[8,512,128]{2,1,0:T(8,128)(2,1)S(1)} custom-call(s32[16,16,32,32]{3,2,1,0:T(8,128)S(1)} %bitcast.12, s32[64,128]{1,0:T(8,128)S(1)} %bitcast.13, s32[72,8,128]{2,1,0:T(8,128)S(1)} %copy-done.3, bf16[6,80]{1,0:T(8,128)(2,1)S(1)} %copy-done.12, bf16[80,80]{1,0:T(8,128)(2,1)S(1)} %copy-done.10, bf16[80,64]{1,0:T(8,128)(2,1)S(1)} %copy.17.last_ref), custom_call_target="tpu_custom_call" | custom-call | tf_op jit(solution)/shard_map/pallas_call | solution.py:243
  77.9 0.0 copy-done.11
  77.9 0.0 copy-done.4
  77.9 0.0 copy-done.9
  77.9 0.0 copy-done.5
  77.9 0.0 copy-done.6
  77.9 0.0 copy-done.7
  77.9 0.0 copy-done.8
  77.9 0.0 copy-start
  77.9 56.4 %shard_map.147.branch_ref = bf16[8,512,128]{2,1,0:T(8,128)(2,1)S(1)} custom-call(bf16[8,512,128]{2,1,0:T(8,128)(2,1)S(1)} %shard_map.146.lat_ref, bf16[2,8,1024,64]{3,2,1,0:T(8,128)(2,1)} %bitcast.14, bf16[256,512]{1,0:T(8,128)(2,1)S(1)} %copy-done.8, bf16[512,256]{1,0:T(8,128)(2,1)S(1)} %copy-done.7, f32[2,16,512]{2,1,0:T(8,128)S(1)} %copy-done.9, ...), custom_call_target="tpu_custom_call" | custom-call | tf_op jit(solution)/shard_map/pallas_call | solution.py:661
  134.3 0.0 copy-done
  134.3 0.0 copy-start.2
  134.3 1.0 copy-done.2
  135.3 5.0 %shard_map.148 = f32[16,4,128,64]{3,2,1,0:T(8,128)} custom-call(bf16[8,512,128]{2,1,0:T(8,128)(2,1)} %copy-done.2, bf16[8,512,128]{2,1,0:T(8,128)(2,1)} %copy-done, bf16[64,64]{1,0:T(8,128)(2,1)} %bitcast.15), custom_call_target="tpu_custom_call" | custom-call | tf_op jit(solution)/shard_map/pallas_call | solution.py:712
  (3 shorter events, 0.0 us)
Async XLA Ops:
  0.0 77.9 %copy-start.11 = (f32[2,512]{1,0:T(2,128)S(1)}, f32[2,512]{1,0:T(2,128)}, u32[]{:S(2)}) copy-start(f32[2,512]{1,0:T(2,128)} %constant.20.clone.lanes_ref) | copy-start | bytes 12292
  0.0 77.9 %copy-start.4 = (bf16[512,512]{1,0:T(8,128)(2,1)S(1)}, bf16[512,512]{1,0:T(8,128)(2,1)}, u32[]{:S(2)}) copy-start(bf16[512,512]{1,0:T(8,128)(2,1)} %constant.19.clone.flip_ref) | copy-start | bytes 1572868
  0.0 77.9 %copy-start.9 = (f32[2,16,512]{2,1,0:T(8,128)S(1)}, f32[2,16,512]{2,1,0:T(8,128)}, u32[]{:S(2)}) copy-start(f32[2,16,512]{2,1,0:T(8,128)} %constant.16.clone.strips_ref) | copy-start | bytes 196612
  18.1 2.2 %copy-start.1 = (s32[1,16,16,32,32]{4,3,2,1,0:T(8,128)S(1)}, s32[1,16,16,32,32]{4,3,2,1,0:T(8,128)}, u32[]{:S(2)}) copy-start(s32[1,16,16,32,32]{4,3,2,1,0:T(8,128)} %param.16) | copy-start | bytes 3145732
  20.3 1.0 copy-start.3
  21.3 0.7 copy-start.10
  22.0 0.7 copy-start.12
  22.7 55.2 %copy-start.5 = (bf16[4,128,256]{2,1,0:T(8,128)(2,1)S(1)}, bf16[4,128,256]{2,1,0:T(8,128)(2,1)}, u32[]{:S(2)}) copy-start(bf16[4,128,256]{2,1,0:T(8,128)(2,1)} %constant.18.clone.back_ref) | copy-start | bytes 786436
  22.7 55.2 %copy-start.6 = (bf16[4,128,256]{2,1,0:T(8,128)(2,1)S(1)}, bf16[4,128,256]{2,1,0:T(8,128)(2,1)}, u32[]{:S(2)}) copy-start(bf16[4,128,256]{2,1,0:T(8,128)(2,1)} %constant.17.clone.ahead_ref) | copy-start | bytes 786436
  22.7 55.2 %copy-start.7 = (bf16[512,256]{1,0:T(8,128)(2,1)S(1)}, bf16[512,256]{1,0:T(8,128)(2,1)}, u32[]{:S(2)}) copy-start(bf16[512,256]{1,0:T(8,128)(2,1)} %constant.15.clone.inverse_ref) | copy-start | bytes 786436
  22.7 55.2 %copy-start.8 = (bf16[256,512]{1,0:T(8,128)(2,1)S(1)}, bf16[256,512]{1,0:T(8,128)(2,1)}, u32[]{:S(2)}) copy-start(bf16[256,512]{1,0:T(8,128)(2,1)} %constant.14.clone.forward_ref) | copy-start | bytes 786436
  77.9 56.4 %copy-start = (bf16[8,512,128]{2,1,0:T(8,128)(2,1)}, bf16[8,512,128]{2,1,0:T(8,128)(2,1)S(1)}, u32[]{:S(2)}) copy-start(bf16[8,512,128]{2,1,0:T(8,128)(2,1)S(1)} %shard_map.146.lat_ref) | copy-start | bytes 3145732
  134.3 1.0 copy-start.2

commit v2 on v1

--- a/solution.py
+++ b/solution.py
@@ -98,55 +98,28 @@
 
 
 def encoder_kernel(
-    sizes, grouped, neighbours_ref, counts_ref, table_ref, in_ref, mid_ref, last_ref, out_ref,
-    codes, first, middle, final, stack, one, two, total,
+    cells, grouped, counts_ref, table_ref, codes, first, middle, final, out_ref,
+    stack, one, two, total,
 ):
-    count_x, count_y, count_z, per_device = sizes
     place_x, place_y, place_z = lax.axis_index("gx"), lax.axis_index("gy"), lax.axis_index("gz")
-    cells_x, cells_y, cells_z, slots = neighbours_ref.shape
+    cells_x, cells_y, cells_z = cells
     rows_y = LANES // cells_z
     rows = counts_ref.shape[0]
-    units = mid_ref.shape[0]
-    channels = last_ref.shape[1]
-    words, table_rows = in_ref.shape[0] // 3, table_ref.shape[0]
+    slots = codes.shape[0] // rows
+    units = middle.shape[0]
+    channels = final.shape[0]
+    words, table_rows = first.shape[1] // (3 * SUB), table_ref.shape[1]
     depth = max(1, (table_rows - 1).bit_length())
     per = stack.shape[0]
     block = total.shape[2] // LANES
     groups = block // SUB
     turns = slots // per
     blocks = rows // block
-
     iota = lambda shape, d: lax.broadcasted_iota(jnp.int32, shape, d)
-    spread = jnp.where(iota((SUB * units, units), 0) % units == iota((SUB * units, units), 1), 1.0, 0.0)
-    values = 3 * words
-    wide = jnp.where(iota((values, values * SUB), 0) == iota((values, values * SUB), 1) // SUB, 1.0, 0.0)
     narrow = lambda a: a.astype(jnp.bfloat16)
-    inputs = in_ref[...].astype(jnp.float32).T
-    tiled = jnp.dot(narrow(inputs), narrow(wide), preferred_element_type=jnp.float32)
-    tiled = jnp.dot(narrow(spread), narrow(tiled), preferred_element_type=jnp.float32)
-    shape = (SUB * units, values * SUB)
-    first[...] = narrow(jnp.where(iota(shape, 0) // units == iota(shape, 1) % SUB, tiled, 0.0))
-    middle[...] = narrow(mid_ref[...].astype(jnp.float32).T * 0.5)
-    turned = narrow(last_ref[...].astype(jnp.float32).T * 0.5)
-    for k in range(per):
-        final[:, units * k : units * (k + 1)] = turned
     one[...] = jnp.zeros_like(one)
     two[...] = jnp.zeros_like(two)
     total[...] = jnp.zeros_like(total)
-    width_y, width_z = min(count_y, 3), min(count_z, 3)
-
-    def prepare(row, carry):
-        strip, x = row // cells_x, lax.rem(row, cells_x)
-        near = neighbours_ref[x, pl.ds(strip * rows_y, rows_y)].reshape(LANES, slots).T
-        owner = over(near, per_device)
-        at_z = offset(within(owner, count_z), place_z, count_z)
-        at_y = offset(within(over(owner, count_z), count_y), place_y, count_y)
-        at_x = offset(over(owner, count_z * count_y), place_x, count_x)
-        code = ((at_x * width_y + at_y) * width_z + at_z) * per_device + within(near, per_device)
-        codes[pl.ds(pl.multiple_of(row * slots, SUB), slots), :] = code
-        return carry
-
-    lax.fori_loop(0, rows, prepare, 0, unroll=min(8, rows))
     lane_ids = iota((SUB, LANES), 1)
     sub_ids = iota((SUB, LANES), 0)
     centre = lambda cell: (cell.astype(jnp.float32) + 0.5) * (1.0 / (GRID * SCALE))
@@ -172,7 +145,7 @@
                 found = []
                 for w in range(words):
                     leaf = lambda r: jnp.take_along_axis(
-                        jnp.broadcast_to(table_ref[r, 3 * w : 3 * w + 1, :], (SUB, LANES)),
+                        jnp.broadcast_to(table_ref[w, r : r + 1, :], (SUB, LANES)),
                         lane,
                         axis=1,
                         mode="promise_in_bounds",
@@ -227,39 +200,46 @@
     lax.fori_loop(0, blocks, close, 0)
 
 
-def encode(neighbours, counts, table, kernel_in, kernel_mid, kernel_out, per_device, grouped):
+def encode(counts, table, codes, first, middle, final, cells, grouped):
     rows = counts.shape[0]
-    slots = neighbours.shape[-1]
-    units, channels = kernel_out.shape
+    units = middle.shape[0]
+    channels = final.shape[0]
     block = min(2 * SUB, rows)
-    per = 2
+    per = final.shape[1] // units
     if grouped:
         shape = jax.ShapeDtypeStruct((channels // SUB, rows * SUB, LANES), jnp.bfloat16)
     else:
         shape = jax.ShapeDtypeStruct((rows, channels, LANES), jnp.float32)
-    sizes = tuple(lax.axis_size(a) for a in ("gx", "gy", "gz")) + (per_device,)
     vmem = lambda: pl.BlockSpec(memory_space=pltpu.VMEM)
-    values = kernel_in.shape[0]
     return pl.pallas_call(
-        functools.partial(encoder_kernel, sizes, grouped),
+        functools.partial(encoder_kernel, cells, grouped),
         out_shape=shape,
         in_specs=[vmem() for _ in range(6)],
         out_specs=vmem(),
         scratch_shapes=[
-            pltpu.VMEM((rows * slots, LANES), jnp.int32),
-            pltpu.VMEM((SUB * units, values * SUB), jnp.bfloat16),
-            pltpu.VMEM((units, units), jnp.bfloat16),
-            pltpu.VMEM((channels, per * units), jnp.bfloat16),
-            pltpu.VMEM((per, values * SUB, block // SUB * LANES), jnp.bfloat16),
+            pltpu.VMEM((per, first.shape[1], block // SUB * LANES), jnp.bfloat16),
             pltpu.VMEM((per, units, block * LANES), jnp.bfloat16),
             pltpu.VMEM((per * units, block * LANES), jnp.bfloat16),
             pltpu.VMEM((rows // block, channels, block * LANES), jnp.float32),
         ],
-        compiler_params=pltpu.CompilerParams(vmem_limit_bytes=40 * 1024 * 1024),
-    )(neighbours, counts, table, kernel_in, kernel_mid, kernel_out)
-
-
-def halo_kernel(sizes, points_ref, out_ref, near, send, recv):
+        compiler_params=pltpu.CompilerParams(vmem_limit_bytes=56 * 1024 * 1024),
+    )(counts, table, codes, first, middle, final)
+
+
+def prepare_kernel(
+    sizes, *refs
+):
+    inputs, refs = refs[:5], refs[5:]
+    out_ref, codes, first, middle, final = refs[:5]
+    near, send, recv, fetched = refs[5:9]
+    local = refs[9:]
+    fetches = [
+        pltpu.make_async_copy(source, target, fetched.at[n])
+        for n, (source, target) in enumerate(zip(inputs, local))
+    ]
+    for fetch in fetches:
+        fetch.start()
+    points_ref, neighbours_ref, in_ref, mid_ref, last_ref = local
     places = [lax.axis_index(a) for a in ("gx", "gy", "gz")]
     widths = [min(n, 3) for n in sizes]
     home = [1 if n > 2 else 0 for n in sizes]
@@ -279,6 +259,7 @@
             barrier, inc=1, device_id=reader(block), device_id_type=pl.DeviceIdType.MESH
         )
     pl.semaphore_wait(barrier, len(others))
+    fetches[0].wait()
     copies = {}
     for block in others:
         b = number(block)
@@ -291,7 +272,45 @@
             device_id_type=pl.DeviceIdType.MESH,
         )
         copies[b].start()
-    pieces = points_ref.shape[1] // LANES
+    place_x, place_y, place_z = places
+    count_x, count_y, count_z = sizes
+    per_device = points_ref.shape[0] * LANES // in_ref.shape[0]
+    cells_x, cells_y, cells_z, slots = neighbours_ref.shape
+    rows_y = LANES // cells_z
+    rows = codes.shape[0] // slots
+    for fetch in fetches[1:]:
+        fetch.wait()
+    units = mid_ref.shape[0]
+    words = in_ref.shape[0] // 3
+    per = final.shape[1] // units
+    iota = lambda shape, d: lax.broadcasted_iota(jnp.int32, shape, d)
+    spread = jnp.where(iota((SUB * units, units), 0) % units == iota((SUB * units, units), 1), 1.0, 0.0)
+    values = 3 * words
+    wide = jnp.where(iota((values, values * SUB), 0) == iota((values, values * SUB), 1) // SUB, 1.0, 0.0)
+    narrow = lambda a: a.astype(jnp.bfloat16)
+    inputs = in_ref[...].astype(jnp.float32).T
+    tiled = jnp.dot(narrow(inputs), narrow(wide), preferred_element_type=jnp.float32)
+    tiled = jnp.dot(narrow(spread), narrow(tiled), preferred_element_type=jnp.float32)
+    shape = (SUB * units, values * SUB)
+    first[...] = narrow(jnp.where(iota(shape, 0) // units == iota(shape, 1) % SUB, tiled, 0.0))
+    middle[...] = narrow(mid_ref[...].astype(jnp.float32).T * 0.5)
+    turned = narrow(last_ref[...].astype(jnp.float32) * 0.5)
+    for k in range(per):
+        final[:, units * k : units * (k + 1)] = turned
+    width_y, width_z = widths[1:]
+    def prepare(row, carry):
+        strip, x = row // cells_x, lax.rem(row, cells_x)
+        near = neighbours_ref[x, pl.ds(strip * rows_y, rows_y)].reshape(LANES, slots).T
+        owner = over(near, per_device)
+        at_z = offset(within(owner, count_z), place_z, count_z)
+        at_y = offset(within(over(owner, count_z), count_y), place_y, count_y)
+        at_x = offset(over(owner, count_z * count_y), place_x, count_x)
+        code = ((at_x * width_y + at_y) * width_z + at_z) * per_device + within(near, per_device)
+        codes[pl.ds(pl.multiple_of(row * slots, SUB), slots), :] = code
+        return carry
+
+    lax.fori_loop(0, rows, prepare, 0, unroll=min(8, rows))
+    pieces = per_device // LANES
     for block in [tuple(home)] + others:
         b = number(block)
         if b in copies:
@@ -299,35 +318,46 @@
             values = near[b]
         else:
             values = points_ref[...]
-        values = jnp.concatenate([values, values[0 : SUB - values.shape[0]]], axis=0)
         fine = jnp.round(values * FINE).astype(jnp.int32)
         coarse = jnp.round(values * COARSE).astype(jnp.int32)
-        for r in range(pieces):
-            part = fine[:, LANES * r : LANES * (r + 1)]
-            third = coarse[:, LANES * r : LANES * (r + 1)]
-            out_ref[b * pieces + r] = (
-                part * 2097152
-                + (pltpu.roll(part, SUB - 1, 0) + 1024) * 1024
-                + (pltpu.roll(third, SUB - 2, 0) + 512)
+        for w in range(words):
+            at = lambda v: slice(pieces * (3 * w + v), pieces * (3 * w + v + 1))
+            out_ref[w, pieces * b : pieces * (b + 1), :] = (
+                fine[at(0)] * 2097152 + (fine[at(1)] + 1024) * 1024 + (coarse[at(2)] + 512)
             )
 
 
-def point_table(points):
+def prepare(points, neighbours, kernel_in, kernel_mid, kernel_out):
     sizes = tuple(lax.axis_size(a) for a in ("gx", "gy", "gz"))
     blocks = math.prod(min(n, 3) for n in sizes)
-    vmem = pl.BlockSpec(memory_space=pltpu.VMEM)
+    units, channels = kernel_out.shape
+    values = kernel_in.shape[0]
+    per = 2
+    vmem = lambda: pl.BlockSpec(memory_space=pltpu.VMEM)
+    shapes = [
+        ((values // 3, blocks * points.size // values // LANES, LANES), jnp.int32),
+        ((neighbours.size // LANES, LANES), jnp.int32),
+        ((SUB * units, values * SUB), jnp.bfloat16),
+        ((units, units), jnp.bfloat16),
+        ((channels, per * units), jnp.bfloat16),
+    ]
+    arrays = (points.reshape(-1, LANES), neighbours, kernel_in, kernel_mid, kernel_out.T)
     return pl.pallas_call(
-        functools.partial(halo_kernel, sizes),
-        out_shape=jax.ShapeDtypeStruct((blocks * points.shape[1] // LANES, SUB, LANES), jnp.int32),
-        in_specs=[vmem],
-        out_specs=vmem,
+        functools.partial(prepare_kernel, sizes),
+        out_shape=[jax.ShapeDtypeStruct(*shape) for shape in shapes],
+        in_specs=[pl.BlockSpec(memory_space=pltpu.HBM) for _ in arrays],
+        out_specs=[vmem() for _ in shapes],
         scratch_shapes=[
-            pltpu.VMEM((blocks,) + points.shape, jnp.float32),
+            pltpu.VMEM((blocks, points.size // LANES, LANES), jnp.float32),
             pltpu.SemaphoreType.DMA((blocks,)),
             pltpu.SemaphoreType.DMA((blocks,)),
-        ],
-        compiler_params=pltpu.CompilerParams(collective_id=1, has_side_effects=True),
-    )(points)
+            pltpu.SemaphoreType.DMA((len(arrays),)),
+        ]
+        + [pltpu.VMEM(a.shape, a.dtype) for a in arrays],
+        compiler_params=pltpu.CompilerParams(
+            collective_id=1, has_side_effects=True, vmem_limit_bytes=62 * 1024 * 1024
+        ),
+    )(*arrays)
 
 
 def lane_maps(quarters, parts, inner_k, inner_j):
@@ -514,24 +544,32 @@
                 arrivals[d, e].wait()
         source = lax.rem(place_y + d, count_y)
         lax.fori_loop(0, chunks, functools.partial(ahead_step, source), 0)
-    whole = plane[...]
-    whole_high, whole_low = split(whole)
-    turn_high, turn_low = split(swap_halves(whole) * sign)
-    table = ahead_ref[place_x]
-    total = jnp.dot(
-        table, jnp.concatenate([whole_high, turn_high], axis=0), preferred_element_type=jnp.float32
-    ) + jnp.dot(
-        table, jnp.concatenate([whole_low, turn_low], axis=0), preferred_element_type=jnp.float32
-    )
+    lane_ids = lax.broadcasted_iota(jnp.int32, (strip_rows, LANES), 1)
     for q in range(count_x):
-        sums[q] = total[:, LANES * q : LANES * (q + 1)]
+        part = plane[:, LANES * q : LANES * (q + 1)]
+        if q == 0:
+            rest = part - part.astype(jnp.bfloat16).astype(jnp.float32)
+            part = jnp.where(lane_ids == LANES // 2, pltpu.roll(rest, LANES // 2, 1), part)
+        sums[q] = part.astype(jnp.bfloat16)
     copies = exchange_with(column, count_x, lambda p: sums.at[p], sums_in.at[place_x], send_b, recv_b)
     sums_in[place_x] = sums[place_x]
     for copy in copies:
         copy.wait()
-    spectrum = sums_in[0]
-    for q in range(1, count_x):
-        spectrum = spectrum + sums_in[q]
+    constant_lane = jnp.logical_and(lane_ids == 0, place_x == 0)
+    rest_lane = jnp.logical_and(lane_ids == LANES // 2, place_x == 0)
+    spectrum = None
+    for q in range(count_x):
+        part = sums_in[q].astype(jnp.float32)
+        part = part + jnp.where(constant_lane, pltpu.roll(part, LANES // 2, 1), 0.0)
+        part = jnp.where(rest_lane, 0.0, part)
+        for piece in split(part):
+            turn = pltpu.roll(piece.astype(jnp.float32), LANES // 2, 1) * sign[:, :LANES]
+            term = jnp.dot(
+                ahead_ref[q],
+                jnp.concatenate([piece, turn.astype(jnp.bfloat16)], axis=0),
+                preferred_element_type=jnp.float32,
+            )
+            spectrum = term if spectrum is None else spectrum + term
     half_rows = half_modes * group
     for z in range(count_z):
         own[z] = spectrum[half_rows * z : half_rows * (z + 1)].astype(jnp.bfloat16)
@@ -666,8 +704,8 @@
         scratch_shapes=[
             pltpu.VMEM(lat.shape, jnp.bfloat16),
             pltpu.VMEM((strip_rows, lanes), jnp.float32),
-            pltpu.VMEM((count_x, MODES * SUB, LANES), jnp.float32),
-            pltpu.VMEM((count_x, MODES * SUB, LANES), jnp.float32),
+            pltpu.VMEM((count_x, strip_rows, LANES), jnp.bfloat16),
+            pltpu.VMEM((count_x, strip_rows, LANES), jnp.bfloat16),
             pltpu.VMEM((count_z, half, LANES), jnp.bfloat16),
             pltpu.VMEM((members, half, LANES), jnp.bfloat16),
             pltpu.VMEM((half_modes, LANES, LANES), jnp.float32),
@@ -690,13 +728,16 @@
 
 
 def final_kernel(branch_ref, lat_ref, skip_ref, out_ref):
-    members, rows, _ = branch_ref.shape
-    count = rows // SUB
-    branch = [branch_ref[p].astype(jnp.float32) for p in range(members)]
-    latent = [lat_ref[p].astype(jnp.float32) for p in range(members)]
+    members = branch_ref.shape[0]
+    count = out_ref.shape[0]
+    rows = count * SUB
+    part = pl.ds(pl.multiple_of(pl.program_id(0) * rows, rows), rows)
+    branch = [branch_ref[p, part, :].astype(jnp.float32) for p in range(members)]
+    latent = [lat_ref[p, part, :].astype(jnp.float32) for p in range(members)]
     pick = lambda parts, x: jnp.concatenate([a[SUB * x : SUB * (x + 1)] for a in parts], axis=0)
     wide = jnp.concatenate([pick(latent, x) for x in range(count)], axis=1).astype(jnp.bfloat16)
-    skip = jnp.dot(skip_ref[...], wide, preferred_element_type=jnp.float32)
+    turned = skip_ref[...].astype(jnp.float32).T.astype(jnp.bfloat16)
+    skip = jnp.dot(turned, wide, preferred_element_type=jnp.float32)
     for x in range(count):
         v = pick(branch, x) + skip[:, LANES * x : LANES * (x + 1)]
         inner = v * (0.7978845608028654 + 0.035677408136300125 * (v * v))
@@ -708,14 +749,15 @@
     members, piece_rows, _ = lat.shape
     channels = skip_weight.shape[0]
     rows = cells_x * SUB
-    piece = pl.BlockSpec((members, rows, LANES), lambda i: (0, i, 0))
+    whole = pl.BlockSpec(memory_space=pltpu.VMEM)
     return pl.pallas_call(
         final_kernel,
         grid=(piece_rows // rows,),
         out_shape=jax.ShapeDtypeStruct((cells_x, piece_rows // rows, LANES, channels), jnp.float32),
-        in_specs=[piece, piece, pl.BlockSpec(skip_weight.shape, lambda i: (0, 0))],
+        in_specs=[whole, whole, whole],
         out_specs=pl.BlockSpec((cells_x, 1, LANES, channels), lambda i: (0, i, 0, 0)),
-    )(branch, lat, skip_weight.T)
+        compiler_params=pltpu.CompilerParams(vmem_limit_bytes=24 * 1024 * 1024),
+    )(branch, lat, skip_weight)
 
 
 def summed_over_axes(values, axes):
@@ -742,6 +784,7 @@
     per_device = point_data.shape[2]
     channels = skip_weight.shape[0]
     rows_y = LANES // cells_z
+    shape = (cells_x, cells_y, cells_z)
     node_order = lambda values: jnp.swapaxes(
         values.reshape(cells_x, cells_y // rows_y, LANES), 0, 1
     ).reshape(-1, LANES)
@@ -755,13 +798,11 @@
     for geometry in range(geometry_count):
         latent.append(
             encode(
-                neighbours[geometry],
                 node_order(counts[geometry]),
-                point_table(point_data[geometry]),
-                kernel_in,
-                kernel_mid,
-                kernel_out,
-                per_device,
+                *prepare(
+                    point_data[geometry], neighbours[geometry], kernel_in, kernel_mid, kernel_out
+                ),
+                shape,
                 grouped,
             )
         )

time: 141 us -> 130 us (0.922)
  local copies, waits for them, and re-layouts: 10.1 us -> 2.99 us
  Pallas kernels: 130 us -> 127 us
    unnamed x29 -> x18, local copies, waits for them, and re-layouts: 9.13 us -> 1.26 us
    pallas_call x1, Pallas kernels: 56.4 us -> 54.2 us  [spectral_branch(): pl.pallas_call(functools.partial(spectral_kernel, count_x, count_y, count...]
where the time goes in v2:
time: 130 us
  Pallas kernels  127 us (98%)
  local copies, waits for them, and re-layouts  2.99 us (2%)
    pallas_call x1, Pallas kernels, encode(): pl.pallas_call(functools.partial(encoder_kernel, cells, grouped), out_sha...  56.5 us
    pallas_call x1, Pallas kernels, spectral_branch(): pl.pallas_call(functools.partial(spectral_kernel, count_x, count_y, count...  54.2 us
    pallas_call x1, Pallas kernels, prepare(): pl.pallas_call(functools.partial(prepare_kernel, sizes), out_shape=[jax.S...  12.2 us
    pallas_call x1, Pallas kernels, finish(): pl.pallas_call(final_kernel, grid=(piece_rows // rows,), out_shape=jax.Sh...  3.82 us

profile of v2, /device:TPU:0, one launch (start us, length us, event | category | flops | bytes accessed | tf_op | source)
XLA Modules:
  0.0 129.8 jit_solution(11452715552155231155)
XLA Ops:
  0.0 0.0 copy-start.8
  0.0 0.0 copy-start.1
  0.0 0.0 copy-start.2
  0.0 0.0 copy-start.3
  0.0 0.0 copy-start.6
  0.0 0.0 copy-start.4
  0.0 0.0 copy-start.5
  0.0 1.1 reshape_squeeze.6
  1.2 0.6 copy.16
  1.8 12.2 %shard_map.145 = (s32[2,72,128]{2,1,0:T(8,128)}, s32[2048,128]{1,0:T(8,128)}, bf16[640,48]{1,0:T(8,128)(2,1)}, bf16[80,80]{1,0:T(8,128)(2,1)}, bf16[64,160]{1,0:T(8,128)(2,1)}) custom-call(f32[24,128]{1,0:T(8,128)} %bitcast.14, s32[16,16,32,32]{3,2,1,0:T(8,128)} %bitcast.11, bf16[6,80]{1,0:T(8,128)(2,1)} %refs_2_.1, bf16[80,80]{1,0:T(8,128)(2,1)} %refs_3_.1, ...), custom_call_target="tpu_custom_call" | custom-call | tf_op jit(solution)/shard_map/pallas_call | solution.py:345
  13.9 56.5 %shard_map.146.lat_ref = bf16[8,512,128]{2,1,0:T(8,128)(2,1)} custom-call(s32[64,128]{1,0:T(8,128)} %bitcast.12, s32[2,72,128]{2,1,0:T(8,128)} %get-tuple-element.10.table_ref, s32[2048,128]{1,0:T(8,128)} %get-tuple-element.11.codes, bf16[640,48]{1,0:T(8,128)(2,1)} %get-tuple-element.12.first, bf16[80,80]{1,0:T(8,128)(2,1)} %get-tuple-element.13.middle, ...), custom_call_target="tpu_custom_call" | custom-call | tf_op jit(solution)/shard_map/pallas_call | solution.py:214
  70.5 0.0 copy-done.8
  70.5 0.0 copy-done.1
  70.5 0.0 copy-done.2
  70.5 0.0 copy-done.3
  70.5 0.0 copy-done.6
  70.5 0.0 copy-done.4
  70.5 0.0 copy-done.5
  70.5 0.0 copy-start
  70.5 1.2 copy-done
  71.7 0.0 copy-start.7
  71.7 54.2 %shard_map.147.branch_ref = bf16[8,512,128]{2,1,0:T(8,128)(2,1)S(1)} custom-call(bf16[8,512,128]{2,1,0:T(8,128)(2,1)S(1)} %copy-done, bf16[2,8,1024,64]{3,2,1,0:T(8,128)(2,1)} %bitcast.10, bf16[256,512]{1,0:T(8,128)(2,1)S(1)} %copy-done.5, bf16[512,256]{1,0:T(8,128)(2,1)S(1)} %copy-done.4, f32[2,16,512]{2,1,0:T(8,128)S(1)} %copy-done.6, ...), custom_call_target="tpu_custom_call" | custom-call | tf_op jit(solution)/shard_map/pallas_call | solution.py:699
  126.0 0.0 copy-done.7
  126.0 3.8 %shard_map.148 = f32[16,4,128,64]{3,2,1,0:T(8,128)} custom-call(bf16[8,512,128]{2,1,0:T(8,128)(2,1)S(1)} %shard_map.147.branch_ref, bf16[8,512,128]{2,1,0:T(8,128)(2,1)S(1)} %copy-done, bf16[64,64]{1,0:T(8,128)(2,1)S(1)} %copy-done.7), custom_call_target="tpu_custom_call" | custom-call | tf_op jit(solution)/shard_map/pallas_call | solution.py:753
Async XLA Ops:
  0.0 70.5 %copy-start.8 = (f32[2,512]{1,0:T(2,128)S(1)}, f32[2,512]{1,0:T(2,128)}, u32[]{:S(2)}) copy-start(f32[2,512]{1,0:T(2,128)} %constant.20.clone.lanes_ref) | copy-start | bytes 12292
  0.0 70.5 %copy-start.1 = (bf16[512,512]{1,0:T(8,128)(2,1)S(1)}, bf16[512,512]{1,0:T(8,128)(2,1)}, u32[]{:S(2)}) copy-start(bf16[512,512]{1,0:T(8,128)(2,1)} %constant.19.clone.flip_ref) | copy-start | bytes 1572868
  0.0 70.5 %copy-start.2 = (bf16[4,128,256]{2,1,0:T(8,128)(2,1)S(1)}, bf16[4,128,256]{2,1,0:T(8,128)(2,1)}, u32[]{:S(2)}) copy-start(bf16[4,128,256]{2,1,0:T(8,128)(2,1)} %constant.18.clone.back_ref) | copy-start | bytes 786436
  0.0 70.5 %copy-start.3 = (bf16[4,128,256]{2,1,0:T(8,128)(2,1)S(1)}, bf16[4,128,256]{2,1,0:T(8,128)(2,1)}, u32[]{:S(2)}) copy-start(bf16[4,128,256]{2,1,0:T(8,128)(2,1)} %constant.17.clone.ahead_ref) | copy-start | bytes 786436
  0.0 70.5 %copy-start.6 = (f32[2,16,512]{2,1,0:T(8,128)S(1)}, f32[2,16,512]{2,1,0:T(8,128)}, u32[]{:S(2)}) copy-start(f32[2,16,512]{2,1,0:T(8,128)} %constant.16.clone.strips_ref) | copy-start | bytes 196612
  0.0 70.5 %copy-start.4 = (bf16[512,256]{1,0:T(8,128)(2,1)S(1)}, bf16[512,256]{1,0:T(8,128)(2,1)}, u32[]{:S(2)}) copy-start(bf16[512,256]{1,0:T(8,128)(2,1)} %constant.15.clone.inverse_ref) | copy-start | bytes 786436
  0.0 70.5 %copy-start.5 = (bf16[256,512]{1,0:T(8,128)(2,1)S(1)}, bf16[256,512]{1,0:T(8,128)(2,1)}, u32[]{:S(2)}) copy-start(bf16[256,512]{1,0:T(8,128)(2,1)} %constant.14.clone.forward_ref) | copy-start | bytes 786436
  70.5 1.2 copy-start
  71.7 54.2 %copy-start.7 = (bf16[64,64]{1,0:T(8,128)(2,1)S(1)}, bf16[64,64]{1,0:T(8,128)(2,1)}, u32[]{:S(2)}) copy-start(bf16[64,64]{1,0:T(8,128)(2,1)} %skip_ref.1) | copy-start | bytes 24580

commit v3 on v2

--- a/solution.py
+++ b/solution.py
@@ -436,7 +436,7 @@
     count_y,
     count_z,
     lat_ref,
-    weight_ref,
+    weight_from,
     forward_ref,
     inverse_ref,
     strips_ref,
@@ -457,6 +457,8 @@
     joined,
     all_modes,
     pieces,
+    weight_ref,
+    fetched,
     send_a, recv_a, send_b, recv_b, send_c, recv_c, send_d, recv_d, send_e, recv_e, send_f, recv_f,
 ):
     place_x, place_y, place_z = lax.axis_index("gx"), lax.axis_index("gy"), lax.axis_index("gz")
@@ -476,6 +478,8 @@
         other = lax.rem(place_x + t, count_x)
         return other, {"gx": other}
 
+    fetch = pltpu.make_async_copy(weight_from, weight_ref, fetched)
+    fetch.start()
     barrier = pltpu.get_barrier_semaphore()
     for t in range(1, members):
         pl.semaphore_signal(barrier, inc=1, device_id=member(t)[1], device_id_type=mesh_id)
@@ -588,6 +592,7 @@
     turned[...] = jnp.zeros_like(turned)
     for copy in copies:
         copy.wait()
+    fetch.wait()
     arrived = [own_in[p].astype(jnp.float32) for p in range(members)]
     for i in range(half_modes):
         column_values = jnp.concatenate([a[group * i : group * (i + 1)] for a in arrived], axis=0)
@@ -699,7 +704,7 @@
     return pl.pallas_call(
         functools.partial(spectral_kernel, count_x, count_y, count_z),
         out_shape=jax.ShapeDtypeStruct(lat.shape, jnp.bfloat16),
-        in_specs=[vmem() for _ in range(9)],
+        in_specs=[vmem(), pl.BlockSpec(memory_space=pltpu.HBM)] + [vmem() for _ in range(7)],
         out_specs=vmem(),
         scratch_shapes=[
             pltpu.VMEM(lat.shape, jnp.bfloat16),
@@ -714,6 +719,8 @@
             pltpu.VMEM((members, half, LANES), jnp.bfloat16),
             pltpu.VMEM((count_x, MODES * SUB, LANES), jnp.bfloat16),
             pltpu.VMEM(lat.shape, jnp.bfloat16),
+            pltpu.VMEM(weight.shape, weight.dtype),
+            dma,
         ]
         + [dma((members,))] * 2
         + [dma((count_x,))] * 2

time: 130 us -> 128 us (0.985)
  Pallas kernels: 127 us -> 125 us
    pallas_call x1, Pallas kernels: 54.2 us -> 52 us  [spectral_branch(): pl.pallas_call(functools.partial(spectral_kernel, count_x, count_y, count...]
where the time goes in v3:
time: 128 us
  Pallas kernels  125 us (98%)
  local copies, waits for them, and re-layouts  2.99 us (2%)
    pallas_call x1, Pallas kernels, encode(): pl.pallas_call(functools.partial(encoder_kernel, cells, grouped), out_sha...  56.5 us
    pallas_call x1, Pallas kernels, spectral_branch(): pl.pallas_call(functools.partial(spectral_kernel, count_x, count_y, count...  52 us
    pallas_call x1, Pallas kernels, prepare(): pl.pallas_call(functools.partial(prepare_kernel, sizes), out_shape=[jax.S...  12.2 us
    pallas_call x1, Pallas kernels, finish(): pl.pallas_call(final_kernel, grid=(piece_rows // rows,), out_shape=jax.Sh...  3.82 us

profile of v3, /device:TPU:0, one launch (start us, length us, event | category | flops | bytes accessed | tf_op | source)
XLA Modules:
  0.0 127.6 jit_solution(3313414760900973376)
XLA Ops:
  0.0 0.0 copy-start.8
  0.0 0.0 copy-start.1
  0.0 0.0 copy-start.2
  0.0 0.0 copy-start.3
  0.0 0.0 copy-start.6
  0.0 0.0 copy-start.4
  0.0 0.0 copy-start.5
  0.0 1.1 reshape_squeeze.6
  1.2 0.6 copy.16
  1.8 12.2 %shard_map.145 = (s32[2,72,128]{2,1,0:T(8,128)}, s32[2048,128]{1,0:T(8,128)}, bf16[640,48]{1,0:T(8,128)(2,1)}, bf16[80,80]{1,0:T(8,128)(2,1)}, bf16[64,160]{1,0:T(8,128)(2,1)}) custom-call(f32[24,128]{1,0:T(8,128)} %bitcast.14, s32[16,16,32,32]{3,2,1,0:T(8,128)} %bitcast.11, bf16[6,80]{1,0:T(8,128)(2,1)} %refs_2_.1, bf16[80,80]{1,0:T(8,128)(2,1)} %refs_3_.1, ...), custom_call_target="tpu_custom_call" | custom-call | tf_op jit(solution)/shard_map/pallas_call | solution.py:345
  13.9 56.5 %shard_map.146.lat_ref = bf16[8,512,128]{2,1,0:T(8,128)(2,1)} custom-call(s32[64,128]{1,0:T(8,128)} %bitcast.12, s32[2,72,128]{2,1,0:T(8,128)} %get-tuple-element.10.table_ref, s32[2048,128]{1,0:T(8,128)} %get-tuple-element.11.codes, bf16[640,48]{1,0:T(8,128)(2,1)} %get-tuple-element.12.first, bf16[80,80]{1,0:T(8,128)(2,1)} %get-tuple-element.13.middle, ...), custom_call_target="tpu_custom_call" | custom-call | tf_op jit(solution)/shard_map/pallas_call | solution.py:214
  70.5 0.0 copy-done.8
  70.5 0.0 copy-done.1
  70.5 0.0 copy-done.2
  70.5 0.0 copy-done.3
  70.5 0.0 copy-done.6
  70.5 0.0 copy-done.4
  70.5 0.0 copy-done.5
  70.5 0.0 copy-start
  70.5 1.2 copy-done
  71.7 0.0 copy-start.7
  71.7 52.0 %shard_map.147.branch_ref = bf16[8,512,128]{2,1,0:T(8,128)(2,1)S(1)} custom-call(bf16[8,512,128]{2,1,0:T(8,128)(2,1)S(1)} %copy-done, bf16[2,8,1024,64]{3,2,1,0:T(8,128)(2,1)} %bitcast.10, bf16[256,512]{1,0:T(8,128)(2,1)S(1)} %copy-done.5, bf16[512,256]{1,0:T(8,128)(2,1)S(1)} %copy-done.4, f32[2,16,512]{2,1,0:T(8,128)S(1)} %copy-done.6, ...), custom_call_target="tpu_custom_call" | custom-call | tf_op jit(solution)/shard_map/pallas_call | solution.py:704
  123.8 0.0 copy-done.7
  123.8 3.8 %shard_map.148 = f32[16,4,128,64]{3,2,1,0:T(8,128)} custom-call(bf16[8,512,128]{2,1,0:T(8,128)(2,1)S(1)} %shard_map.147.branch_ref, bf16[8,512,128]{2,1,0:T(8,128)(2,1)S(1)} %copy-done, bf16[64,64]{1,0:T(8,128)(2,1)S(1)} %copy-done.7), custom_call_target="tpu_custom_call" | custom-call | tf_op jit(solution)/shard_map/pallas_call | solution.py:760
Async XLA Ops:
  0.0 70.5 %copy-start.8 = (f32[2,512]{1,0:T(2,128)S(1)}, f32[2,512]{1,0:T(2,128)}, u32[]{:S(2)}) copy-start(f32[2,512]{1,0:T(2,128)} %constant.20.clone.lanes_ref) | copy-start | bytes 12292
  0.0 70.5 %copy-start.1 = (bf16[512,512]{1,0:T(8,128)(2,1)S(1)}, bf16[512,512]{1,0:T(8,128)(2,1)}, u32[]{:S(2)}) copy-start(bf16[512,512]{1,0:T(8,128)(2,1)} %constant.19.clone.flip_ref) | copy-start | bytes 1572868
  0.0 70.5 %copy-start.2 = (bf16[4,128,256]{2,1,0:T(8,128)(2,1)S(1)}, bf16[4,128,256]{2,1,0:T(8,128)(2,1)}, u32[]{:S(2)}) copy-start(bf16[4,128,256]{2,1,0:T(8,128)(2,1)} %constant.18.clone.back_ref) | copy-start | bytes 786436
  0.0 70.5 %copy-start.3 = (bf16[4,128,256]{2,1,0:T(8,128)(2,1)S(1)}, bf16[4,128,256]{2,1,0:T(8,128)(2,1)}, u32[]{:S(2)}) copy-start(bf16[4,128,256]{2,1,0:T(8,128)(2,1)} %constant.17.clone.ahead_ref) | copy-start | bytes 786436
  0.0 70.5 %copy-start.6 = (f32[2,16,512]{2,1,0:T(8,128)S(1)}, f32[2,16,512]{2,1,0:T(8,128)}, u32[]{:S(2)}) copy-start(f32[2,16,512]{2,1,0:T(8,128)} %constant.16.clone.strips_ref) | copy-start | bytes 196612
  0.0 70.5 %copy-start.4 = (bf16[512,256]{1,0:T(8,128)(2,1)S(1)}, bf16[512,256]{1,0:T(8,128)(2,1)}, u32[]{:S(2)}) copy-start(bf16[512,256]{1,0:T(8,128)(2,1)} %constant.15.clone.inverse_ref) | copy-start | bytes 786436
  0.0 70.5 %copy-start.5 = (bf16[256,512]{1,0:T(8,128)(2,1)S(1)}, bf16[256,512]{1,0:T(8,128)(2,1)}, u32[]{:S(2)}) copy-start(bf16[256,512]{1,0:T(8,128)(2,1)} %constant.14.clone.forward_ref) | copy-start | bytes 786436
  70.5 1.2 copy-start
  71.7 52.0 %copy-start.7 = (bf16[64,64]{1,0:T(8,128)(2,1)S(1)}, bf16[64,64]{1,0:T(8,128)(2,1)}, u32[]{:S(2)}) copy-start(bf16[64,64]{1,0:T(8,128)(2,1)} %skip_ref.1) | copy-start | bytes 24580
